TPU v7x, 256 devices: a whole 4x4x8 slice. The times are simulated.
256 devices in a mesh: expert: 8 (over x, core), shard: 32 (over z, y).
Axes of the slice: x: 4, y: 4, z: 8, core: 2. Of those that a mesh axis runs over, the one named last changes fastest.
Arguments:
- master_gate: float32 [128, 2048, 768], P('expert', 'shard'), may hold values from -0.125 to 0.125
- master_up: float32 [128, 2048, 768], P('expert', 'shard'), may hold values from -0.125 to 0.125
- router_weight: float32 [2048, 128], P('shard', 'expert'), may hold values from -0.125 to 0.125
- router_gain: float32 [2048], P('shard'), may hold values from 0.25 to 1.75
Outputs:
- final_gate: bfloat16 [128, 768, 2048], P('expert', 'shard')
- final_up: bfloat16 [128, 768, 2048], P('expert', 'shard')
- serve_router: bfloat16 [2048, 128], replicated
All inputs are finite; a program needn't handle non-finite values.
Results may differ from a plain program's by a relative error of at most 0.001.
Values may be sent and summed in bfloat16 or wider, within the bound.
No kernel may reach another device: no remote copies, remote signals or barrier semaphores. Data moves between devices by JAX's collectives and lax.ppermute only.
A program may use at most 64 MiB of HBM per device.

v0:
```python
import functools

import jax
import jax.numpy as jnp
from jax import lax
from jax.experimental import pallas as pl
from jax.experimental.pallas import tpu as pltpu
from jax.sharding import Mesh
from jax.sharding import PartitionSpec as P

EXPERT = ("x", "core")
SHARD = ("z", "y")
RINGED = 6
LANES = 128
TILE = 8

VMEM = pl.BlockSpec(memory_space=pltpu.VMEM)
GRANT = pltpu.CompilerParams(vmem_limit_bytes=16 * 2**20)
RING_ORDER = (3, 5, 4, 2, 6, 1, 7)
SIDE_ORDER = (1, 3, 2)


def two_experts(master_ref):
    swap = lax.axis_index("y") % 2
    stacked = jnp.concatenate([master_ref[swap, 0], master_ref[1 - swap, 0]], axis=0)
    return stacked.astype(jnp.bfloat16).T


def merged_pairs(first, second):
    low = lax.broadcasted_iota(jnp.int32, first.shape, first.ndim - 1) < LANES // 2
    here = jnp.where(low, first, second)
    there = jnp.where(low, second, first)
    return here, jnp.concatenate([there[..., LANES // 2 :], there[..., : LANES // 2]], axis=-1)


def pack_ringed_kernel(zs, ys, own, master_ref, weight_ref, gain_ref, *refs):
    outs, rows_ref = refs[:zs], refs[zs]
    step = pl.program_id(0)
    z = lax.axis_index("z")
    rows_ref[...] = two_experts(master_ref)
    for dz in range(zs):
        start = lax.rem(z + dz, zs) * (ys * own)
        moved = rows_ref[pl.ds(pl.multiple_of(start, TILE), ys * own), :]
        for y in range(ys):
            row = pl.multiple_of((y * RINGED + step) * own, TILE)
            outs[dz][pl.ds(row, own), :] = moved[y * own : (y + 1) * own]

    @pl.when(step == 0)
    def _():
        part = (weight_ref[...] * gain_ref[...]).astype(jnp.bfloat16)
        tile = jnp.concatenate([part[:TILE], part[TILE:]], axis=1)
        for out in outs:
            out[-TILE:, :] = tile


def pack_ringed(master, weight, gain, zs, ys):
    _, _, depth, wide = master.shape
    own = wide // (zs * ys)
    return pl.pallas_call(
        functools.partial(pack_ringed_kernel, zs, ys, own),
        grid=(RINGED,),
        in_specs=[
            pl.BlockSpec((2, 1, depth, wide), lambda e: (0, e, 0, 0)),
            pl.BlockSpec(weight.shape, lambda e: (0, 0)),
            pl.BlockSpec(gain.shape, lambda e: (0, 0)),
        ],
        out_specs=[VMEM] * zs,
        out_shape=[jax.ShapeDtypeStruct((ys * RINGED * own + TILE, LANES), jnp.bfloat16)] * zs,
        scratch_shapes=[pltpu.VMEM((wide, LANES), jnp.bfloat16)],
        compiler_params=GRANT,
        cost_estimate=pl.CostEstimate(flops=10**8, bytes_accessed=10**7, transcendentals=0),
        name="pack_ringed",
    )(master, weight, gain)


def router_tiles_kernel(*refs):
    zs = len(refs) - 1
    z = lax.axis_index("z")
    for j in range(zs):
        refs[zs][lax.rem(z + zs - j, zs)] = refs[j][-TILE:, :]


def router_tiles(near):
    return pl.pallas_call(
        router_tiles_kernel,
        in_specs=[VMEM] * len(near),
        out_specs=VMEM,
        out_shape=jax.ShapeDtypeStruct((len(near), TILE, LANES), jnp.bfloat16),
        compiler_params=GRANT,
        name="router_tiles",
    )(*near)


def regroup_kernel(ys, *refs):
    zs = len(refs) - ys
    z, y = lax.axis_index("z"), lax.axis_index("y")
    rows = (refs[0].shape[0] - TILE) // ys
    for k in range(ys):
        start = pl.multiple_of(lax.rem(y + k, ys) * rows, TILE)
        for j in range(zs):
            refs[zs + k][lax.rem(z + zs - j, zs)] = refs[j][pl.ds(start, rows), :]


def regroup(near, ys):
    rows, lanes = near[0].shape
    shape = jax.ShapeDtypeStruct((len(near), (rows - TILE) // ys, lanes), jnp.bfloat16)
    return pl.pallas_call(
        functools.partial(regroup_kernel, ys),
        in_specs=[VMEM] * len(near),
        out_specs=[VMEM] * ys,
        out_shape=[shape] * ys,
        compiler_params=GRANT,
        name="regroup",
    )(*near)


def for_each_y(ys, write):
    y = lax.axis_index("y")
    for me in range(ys):

        @pl.when(y == me)
        def _():
            for even in range(0, ys, 2):
                write(even, (me - even) % ys, (me - even - 1) % ys)


def router_rows_kernel(*refs):
    out_ref = refs[-1]
    ys = len(refs) - 1

    def write(even, a, b):
        for z in range(refs[0].shape[0]):
            first, second = refs[a][z], refs[b][z]
            column = (z * ys + even) * (LANES // 2)
            out_ref[:TILE, column : column + LANES] = jnp.concatenate(
                [first[:, : LANES // 2], second[:, : LANES // 2]], axis=1
            )
            out_ref[TILE:, column : column + LANES] = jnp.concatenate(
                [first[:, LANES // 2 :], second[:, LANES // 2 :]], axis=1
            )

    for_each_y(ys, write)


def router_rows(tiles):
    zs, ys = tiles[0].shape[0], len(tiles)
    return pl.pallas_call(
        router_rows_kernel,
        in_specs=[VMEM] * ys,
        out_specs=VMEM,
        out_shape=jax.ShapeDtypeStruct((2 * TILE, zs * ys * LANES // 2), jnp.bfloat16),
        compiler_params=GRANT,
        name="router_rows",
    )(*tiles)


def unpack_ringed_kernel(own, *refs):
    out_ref = refs[-1]
    ys = len(refs) - 1
    rows = pl.ds(pl.multiple_of(pl.program_id(0) * own, TILE), own)

    def write(even, a, b):
        for z in range(refs[0].shape[0]):
            column = (z * ys + even) * (LANES // 2)
            here, there = merged_pairs(refs[a][z, rows, :], refs[b][z, rows, :])
            out_ref[0, 0, :, column : column + LANES] = here
            out_ref[1, 0, :, column : column + LANES] = there

    for_each_y(ys, write)


def unpack_ringed(groups, half, own):
    zs, ys = groups[0].shape[0], len(groups)
    depth = zs * ys * LANES // 2
    return pl.pallas_call(
        functools.partial(unpack_ringed_kernel, own),
        grid=(RINGED,),
        in_specs=[VMEM] * ys,
        out_specs=pl.BlockSpec((2, 1, own, depth), lambda e: (0, e, 0, 0)),
        out_shape=jax.ShapeDtypeStruct((2, half, own, depth), jnp.bfloat16),
        compiler_params=GRANT,
        cost_estimate=pl.CostEstimate(flops=10**8, bytes_accessed=10**7, transcendentals=0),
        name="unpack_ringed",
    )(*groups)


def pack_rest_kernel(left, shards, own, gate_ref, up_ref, out_ref):
    step = pl.program_id(0)
    rows = pl.ds(pl.multiple_of(step * own, TILE), own)

    @pl.when(step < left)
    def _():
        out_ref[:, rows, :] = two_experts(gate_ref).reshape(shards, own, LANES)

    @pl.when(step >= left)
    def _():
        out_ref[:, rows, :] = two_experts(up_ref).reshape(shards, own, LANES)


def pack_rest(gate, up, shards):
    _, half, depth, wide = gate.shape
    own, left = wide // shards, half - RINGED
    return pl.pallas_call(
        functools.partial(pack_rest_kernel, left, shards, own),
        grid=(left + half,),
        in_specs=[
            pl.BlockSpec((2, 1, depth, wide), lambda e: (0, jnp.minimum(RINGED + e, half - 1), 0, 0)),
            pl.BlockSpec((2, 1, depth, wide), lambda e: (0, jnp.maximum(e - left, 0), 0, 0)),
        ],
        out_specs=VMEM,
        out_shape=pltpu.HBM((shards, (left + half) * own, LANES), jnp.bfloat16),
        compiler_params=GRANT,
        cost_estimate=pl.CostEstimate(flops=10**8, bytes_accessed=10**7, transcendentals=0),
        name="pack_rest",
    )(gate, up)


def unpack_rest_kernel(left, own, in_ref, _, gate_ref, up_ref):
    step = pl.program_id(0)
    rows = pl.ds(pl.multiple_of(step * own, TILE), own)

    def write(out_ref):
        for k in range(in_ref.shape[0] // 2):
            here, there = merged_pairs(in_ref[2 * k, rows, :], in_ref[2 * k + 1, rows, :])
            out_ref[0, 0, :, k * LANES : (k + 1) * LANES] = here
            out_ref[1, 0, :, k * LANES : (k + 1) * LANES] = there

    @pl.when(step < left)
    def _():
        write(gate_ref)

    @pl.when(step >= left)
    def _():
        write(up_ref)


def unpack_rest(received, gate):
    _, half, own, depth = gate.shape
    left = half - RINGED
    return pl.pallas_call(
        functools.partial(unpack_rest_kernel, left, own),
        grid=(left + half,),
        in_specs=[VMEM, pl.BlockSpec(memory_space=pl.ANY)],
        out_specs=[
            pl.BlockSpec((2, 1, own, depth), lambda e: (0, jnp.minimum(RINGED + e, half - 1), 0, 0)),
            pl.BlockSpec((2, 1, own, depth), lambda e: (0, jnp.maximum(e - left, 0), 0, 0)),
        ],
        out_shape=[jax.ShapeDtypeStruct(gate.shape, jnp.bfloat16)] * 2,
        input_output_aliases={1: 0},
        compiler_params=GRANT,
        cost_estimate=pl.CostEstimate(flops=10**8, bytes_accessed=10**7, transcendentals=0),
        name="unpack_rest",
    )(received, gate)


def in_hbm(array):
    return pltpu.with_memory_space_constraint(array, pltpu.HBM)


def shifted(block, axis, by):
    size = lax.axis_size(axis)
    return lax.ppermute(block, axis, [(k, (k + by) % size) for k in range(size)])


def per_device(master_gate, master_up, router_weight, router_gain):
    zs, ys = lax.axis_size("z"), lax.axis_size("y")
    experts, depth, wide = master_gate.shape
    half, own = experts // 2, wide // (zs * ys)
    gate, up = (m.reshape(2, half, depth, wide) for m in (master_gate, master_up))
    gate = in_hbm(gate)
    weight, gain = in_hbm(router_weight.T), in_hbm(router_gain[None])
    near = list(pack_ringed(gate, weight, gain, zs, ys))
    for dz in RING_ORDER:
        near[dz] = shifted(near[dz], "z", dz)
    rest = pack_rest(gate, up, zs * ys)
    got_rest = lax.all_to_all(rest, SHARD, 0, 0, tiled=True)
    tiles = [router_tiles(near)] * ys
    for dy in SIDE_ORDER:
        tiles[dy] = shifted(tiles[dy], "y", dy)
    groups = list(regroup(near, ys))
    for dy in SIDE_ORDER:
        groups[dy] = shifted(groups[dy], "y", dy)
    everyone = lax.all_gather(router_rows(tiles), EXPERT, axis=0, tiled=True)
    serve_router = everyone.T
    final_gate = unpack_ringed(groups, half, own)
    final_gate, final_up = unpack_rest(got_rest, final_gate)
    whole = (experts, own, zs * ys * depth)
    return final_gate.reshape(whole), final_up.reshape(whole), serve_router


def solution(mesh):
    torus = Mesh(mesh.devices.reshape(4, 2, 8, 4), ("x", "core", "z", "y"))
    return jax.shard_map(
        per_device,
        mesh=torus,
        in_specs=(P(EXPERT, SHARD, None), P(EXPERT, SHARD, None), P(SHARD, EXPERT), P(SHARD)),
        out_specs=(P(EXPERT, SHARD, None), P(EXPERT, SHARD, None), P()),
        check_vma=False,
    )
```

profile of v0, /device:TPU:1, one launch (start us, length us, event | category | flops | bytes accessed | tf_op | source)
XLA Modules:
  0.0 137.4 jit_solution(1312101762511778656)
XLA Ops:
  0.6 1.9 %copy-done = f32[16,64,768]{2,1,0:T(8,128)S(1)} copy-done((f32[16,64,768]{2,1,0:T(8,128)S(1)}, f32[16,64,768]{2,1,0:T(8,128)}, u32[]{:S(2)}) %copy-start) | copy-done | bytes 3145752
  2.5 4.0 %pack_rest.1 = bf16[32,240,128]{2,1,0:T(8,128)(2,1)} custom-call(f32[2,8,64,768]{3,2,1,0:T(8,128)} %bitcast.8, f32[2,8,64,768]{3,2,1,0:T(8,128)S(1)} %bitcast.7), custom_call_target="tpu_custom_call" | custom-call | flops 100000000 | bytes 10000000 | tf_op jit(solution)/shard_map/pack_rest/pallas_call | solution.py:203
  6.5 12.0 %all-to-all-start = ((bf16[32,240,128]{2,1,0:T(8,128)(2,1)}), bf16[32,240,128]{2,1,0:T(8,128)(2,1)S(1)}, u32[]{:S(2)}, u32[]{:S(2)}) async-start(bf16[32,240,128]{2,1,0:T(8,128)(2,1)} %pack_rest.1), calls=%async_computation | async-start | bytes 3932160 | tf_op jit(solution)/shard_map/all_to_all | solution.py:276
  18.5 3.7 %pack_ringed.1 = (bf16[584,128]{1,0:T(8,128)(2,1)S(1)}, bf16[584,128]{1,0:T(8,128)(2,1)S(1)}, bf16[584,128]{1,0:T(8,128)(2,1)S(1)}, bf16[584,128]{1,0:T(8,128)(2...) custom-call(f32[2,8,64,768]{3,2,1,0:T(8,128)} %bitcast.9, ...), custom_call_target="tpu_custom_call" | custom-call | flops 100000000 | bytes 10000000 | tf_op jit(solution)/shard_map/pack_ringed/pallas_call | solution.py:59
  22.2 1.3 collective-permute-start
  23.6 2.1 %collective-permute-start.1 = (bf16[584,128]{1,0:T(8,128)(2,1)S(1)}, bf16[584,128]{1,0:T(8,128)(2,1)S(1)}, u32[]{:S(2)}, u32[]{:S(2)}) collective-permute-start(bf16[584,128]{1,0:T(8,128)(2,1)S(1)} %get-tuple-element.19), channel_id=1, source_target_pairs={{0,8},{4,12},{8,16},{12,20},{16,24},{20,28},{24,0},{28,4},{1,9},{5... | collective-permute-start | bytes 448520 | tf_op jit(solution)/shard_map/ppermute | solution.py:262
  25.6 2.5 %collective-permute-start.2 = (bf16[584,128]{1,0:T(8,128)(2,1)S(1)}, bf16[584,128]{1,0:T(8,128)(2,1)S(1)}, u32[]{:S(2)}, u32[]{:S(2)}) collective-permute-start(bf16[584,128]{1,0:T(8,128)(2,1)S(1)} %get-tuple-element.20), channel_id=1, source_target_pairs={{0,12},{4,16},{8,20},{12,24},{16,28},{20,0},{24,4},{28,8},{1,13},{... | collective-permute-start | bytes 448520 | tf_op jit(solution)/shard_map/ppermute | solution.py:262
  28.1 2.0 %collective-permute-start.3 = (bf16[584,128]{1,0:T(8,128)(2,1)S(1)}, bf16[584,128]{1,0:T(8,128)(2,1)S(1)}, u32[]{:S(2)}, u32[]{:S(2)}) collective-permute-start(bf16[584,128]{1,0:T(8,128)(2,1)S(1)} %get-tuple-element.21), channel_id=1, source_target_pairs={{0,16},{4,20},{8,24},{12,28},{16,0},{20,4},{24,8},{28,12},{1,17},{... | collective-permute-start | bytes 448520 | tf_op jit(solution)/shard_map/ppermute | solution.py:262
  30.1 2.5 %collective-permute-start.4 = (bf16[584,128]{1,0:T(8,128)(2,1)S(1)}, bf16[584,128]{1,0:T(8,128)(2,1)S(1)}, u32[]{:S(2)}, u32[]{:S(2)}) collective-permute-start(bf16[584,128]{1,0:T(8,128)(2,1)S(1)} %get-tuple-element.22), channel_id=1, source_target_pairs={{0,20},{4,24},{8,28},{12,0},{16,4},{20,8},{24,12},{28,16},{1,21},{... | collective-permute-start | bytes 448520 | tf_op jit(solution)/shard_map/ppermute | solution.py:262
  32.6 33.9 %collective-permute-done.refs_1_ = bf16[584,128]{1,0:T(8,128)(2,1)S(1)} collective-permute-done((bf16[584,128]{1,0:T(8,128)(2,1)S(1)}, bf16[584,128]{1,0:T(8,128)(2,1)S(1)}, u32[]{:S(2)}, u32[]{:S(2)}) %collective-permute-start) | collective-permute-done | bytes 149536 | tf_op jit(solution)/shard_map/ppermute | solution.py:262
  66.5 2.3 %collective-permute-start.5 = (bf16[584,128]{1,0:T(8,128)(2,1)S(1)}, bf16[584,128]{1,0:T(8,128)(2,1)S(1)}, u32[]{:S(2)}, u32[]{:S(2)}) collective-permute-start(bf16[584,128]{1,0:T(8,128)(2,1)S(1)} %get-tuple-element.23), channel_id=1, source_target_pairs={{0,24},{4,28},{8,0},{12,4},{16,8},{20,12},{24,16},{28,20},{1,25},{... | collective-permute-start | bytes 448520 | tf_op jit(solution)/shard_map/ppermute | solution.py:262
  68.7 3.6 %collective-permute-done.1.refs_2_ = bf16[584,128]{1,0:T(8,128)(2,1)S(1)} collective-permute-done((bf16[584,128]{1,0:T(8,128)(2,1)S(1)}, bf16[584,128]{1,0:T(8,128)(2,1)S(1)}, u32[]{:S(2)}, u32[]{:S(2)}) %collective-permute-start.1) | collective-permute-done | bytes 149536 | tf_op jit(solution)/shard_map/ppermute | solution.py:262
  72.4 1.9 %collective-permute-start.6 = (bf16[584,128]{1,0:T(8,128)(2,1)S(1)}, bf16[584,128]{1,0:T(8,128)(2,1)S(1)}, u32[]{:S(2)}, u32[]{:S(2)}) collective-permute-start(bf16[584,128]{1,0:T(8,128)(2,1)S(1)} %get-tuple-element.24), channel_id=1, source_target_pairs={{0,28},{4,0},{8,4},{12,8},{16,12},{20,16},{24,20},{28,24},{1,29},{... | collective-permute-start | bytes 448520 | tf_op jit(solution)/shard_map/ppermute | solution.py:262
  74.2 10.0 %collective-permute-done.2.refs_3_ = bf16[584,128]{1,0:T(8,128)(2,1)S(1)} collective-permute-done((bf16[584,128]{1,0:T(8,128)(2,1)S(1)}, bf16[584,128]{1,0:T(8,128)(2,1)S(1)}, u32[]{:S(2)}, u32[]{:S(2)}) %collective-permute-start.2) | collective-permute-done | bytes 149536 | tf_op jit(solution)/shard_map/ppermute | solution.py:262
  84.2 5.2 %collective-permute-done.3.refs_4_ = bf16[584,128]{1,0:T(8,128)(2,1)S(1)} collective-permute-done((bf16[584,128]{1,0:T(8,128)(2,1)S(1)}, bf16[584,128]{1,0:T(8,128)(2,1)S(1)}, u32[]{:S(2)}, u32[]{:S(2)}) %collective-permute-start.3) | collective-permute-done | bytes 149536 | tf_op jit(solution)/shard_map/ppermute | solution.py:262
  90.4 1.3 collective-permute-start.7
  91.7 3.0 %collective-permute-start.8 = (bf16[8,144,128]{2,1,0:T(8,128)(2,1)}, bf16[8,144,128]{2,1,0:T(8,128)(2,1)S(1)}, u32[]{:S(2)}, u32[]{:S(2)}) collective-permute-start(bf16[8,144,128]{2,1,0:T(8,128)(2,1)} %get-tuple-element.27), channel_id=1, source_target_pairs={{0,2},{1,3},{2,0},{3,1},{4,6},{5,7},{6,4},{7,5},{8,10},{9,11},{10,... | collective-permute-start | bytes 884744 | tf_op jit(solution)/shard_map/ppermute | solution.py:262
  96.0 2.1 %collective-permute-start.11 = (bf16[8,8,128]{2,1,0:T(8,128)(2,1)S(1)}, bf16[8,8,128]{2,1,0:T(8,128)(2,1)S(1)}, u32[]{:S(2)}, u32[]{:S(2)}) collective-permute-start(bf16[8,8,128]{2,1,0:T(8,128)(2,1)S(1)} %router_tiles.1.refs_0_), channel_id=1, source_target_pairs={{0,2},{1,3},{2,0},{3,1},{4,6},{5,7},{6,4},{7,5},{8,10},{9,11},{10,... | collective-permute-start | bytes 49160 | tf_op jit(solution)/shard_map/ppermute | solution.py:262
  98.1 9.4 %collective-permute-done.12.refs_3_ = bf16[8,8,128]{2,1,0:T(8,128)(2,1)S(1)} collective-permute-done((bf16[8,8,128]{2,1,0:T(8,128)(2,1)S(1)}, bf16[8,8,128]{2,1,0:T(8,128)(2,1)S(1)}, u32[]{:S(2)}, u32[]{:S(2)}) %collective-permute-start.12) | collective-permute-done | bytes 16416 | tf_op jit(solution)/shard_map/ppermute | solution.py:262
  108.7 3.5 %collective-permute-done.10.refs_1_ = bf16[8,8,128]{2,1,0:T(8,128)(2,1)S(1)} collective-permute-done((bf16[8,8,128]{2,1,0:T(8,128)(2,1)S(1)}, bf16[8,8,128]{2,1,0:T(8,128)(2,1)S(1)}, u32[]{:S(2)}, u32[]{:S(2)}) %collective-permute-start.10) | collective-permute-done | bytes 16416 | tf_op jit(solution)/shard_map/ppermute | solution.py:262
  112.3 16.3 %all_gather.3 = bf16[128,2048]{1,0:T(8,128)(2,1)} all-gather(bf16[16,2048]{1,0:T(8,128)(2,1)S(1)} %router_rows.1), channel_id=1, replica_groups=mesh['x'=4,'core'=2,'z'=8,'y'=4] {'x','core'}, dimensions={0}, use_global_device_ids=true | all-gather | bytes 589824 | tf_op jit(solution)/shard_map/all_gather | solution.py:283
  128.6 2.0 %copy.8 = bf16[2048,128]{1,0:T(8,128)(2,1)} copy(bf16[2048,128]{0,1:T(8,128)(2,1)} %bitcast.11) | data formatting | bytes 1048576
  130.7 2.6 %unpack_ringed.1._ = bf16[2,8,24,2048]{3,2,1,0:T(8,128)(2,1)} custom-call(bf16[8,144,128]{2,1,0:T(8,128)(2,1)S(1)} %get-tuple-element.25.refs_0_, bf16[8,144,128]{2,1,0:T(8,128)(2,1)S(1)} %collective-permute-done.7.refs_1_, bf16[8,144,128]{2,1,0:T(8,128)(2,1)S(1)} %collective-permute-done.8.refs_2_, bf16[8,144,128]{2,1,0:T(8,128)(2,1)S(1)} %collective-permute-done.9.refs_3_), custom_call_target="tpu_custom_call" | custom-call | flops 100000000 | bytes 10000000 | tf_op jit(solution)/shard_map/unpack_ringed/pallas_call | solution.py:175
  133.3 4.2 %unpack_rest.1 = (bf16[2,8,24,2048]{3,2,1,0:T(8,128)(2,1)}, bf16[2,8,24,2048]{3,2,1,0:T(8,128)(2,1)}) custom-call(bf16[32,240,128]{2,1,0:T(8,128)(2,1)S(1)} %all-to-all-done.in_ref, bf16[2,8,24,2048]{3,2,1,0:T(8,128)(2,1)} %unpack_ringed.1._), custom_call_target="tpu_custom_call", output_to_operand_aliasing={{0}: (1, {})} | custom-call | flops 100000000 | bytes 10000000 | tf_op jit(solution)/shard_map/unpack_rest/pallas_call | solution.py:240
  (15 shorter events, 3.5 us)
Async XLA Ops:
  0.6 1.9 %copy-start = (f32[16,64,768]{2,1,0:T(8,128)S(1)}, f32[16,64,768]{2,1,0:T(8,128)}, u32[]{:S(2)}) copy-start(f32[16,64,768]{2,1,0:T(8,128)} %param.5) | copy-start | bytes 9437188
  6.5 126.8 %all-to-all-start = ((bf16[32,240,128]{2,1,0:T(8,128)(2,1)}), bf16[32,240,128]{2,1,0:T(8,128)(2,1)S(1)}, u32[]{:S(2)}, u32[]{:S(2)}) async-start(bf16[32,240,128]{2,1,0:T(8,128)(2,1)} %pack_rest.1), calls=%async_computation | async-start | bytes 3932160 | tf_op jit(solution)/shard_map/all_to_all | solution.py:276
  22.2 44.2 %collective-permute-start = (bf16[584,128]{1,0:T(8,128)(2,1)S(1)}, bf16[584,128]{1,0:T(8,128)(2,1)S(1)}, u32[]{:S(2)}, u32[]{:S(2)}) collective-permute-start(bf16[584,128]{1,0:T(8,128)(2,1)S(1)} %get-tuple-element.18), channel_id=1, source_target_pairs={{0,4},{4,8},{8,12},{12,16},{16,20},{20,24},{24,28},{28,0},{1,5},{5... | collective-permute-start | bytes 448520 | tf_op jit(solution)/shard_map/ppermute | solution.py:262
  23.6 48.8 %collective-permute-start.1 = (bf16[584,128]{1,0:T(8,128)(2,1)S(1)}, bf16[584,128]{1,0:T(8,128)(2,1)S(1)}, u32[]{:S(2)}, u32[]{:S(2)}) collective-permute-start(bf16[584,128]{1,0:T(8,128)(2,1)S(1)} %get-tuple-element.19), channel_id=1, source_target_pairs={{0,8},{4,12},{8,16},{12,20},{16,24},{20,28},{24,0},{28,4},{1,9},{5... | collective-permute-start | bytes 448520 | tf_op jit(solution)/shard_map/ppermute | solution.py:262
  25.6 58.6 %collective-permute-start.2 = (bf16[584,128]{1,0:T(8,128)(2,1)S(1)}, bf16[584,128]{1,0:T(8,128)(2,1)S(1)}, u32[]{:S(2)}, u32[]{:S(2)}) collective-permute-start(bf16[584,128]{1,0:T(8,128)(2,1)S(1)} %get-tuple-element.20), channel_id=1, source_target_pairs={{0,12},{4,16},{8,20},{12,24},{16,28},{20,0},{24,4},{28,8},{1,13},{... | collective-permute-start | bytes 448520 | tf_op jit(solution)/shard_map/ppermute | solution.py:262
  28.1 61.3 %collective-permute-start.3 = (bf16[584,128]{1,0:T(8,128)(2,1)S(1)}, bf16[584,128]{1,0:T(8,128)(2,1)S(1)}, u32[]{:S(2)}, u32[]{:S(2)}) collective-permute-start(bf16[584,128]{1,0:T(8,128)(2,1)S(1)} %get-tuple-element.21), channel_id=1, source_target_pairs={{0,16},{4,20},{8,24},{12,28},{16,0},{20,4},{24,8},{28,12},{1,17},{... | collective-permute-start | bytes 448520 | tf_op jit(solution)/shard_map/ppermute | solution.py:262
  30.1 59.3 %collective-permute-start.4 = (bf16[584,128]{1,0:T(8,128)(2,1)S(1)}, bf16[584,128]{1,0:T(8,128)(2,1)S(1)}, u32[]{:S(2)}, u32[]{:S(2)}) collective-permute-start(bf16[584,128]{1,0:T(8,128)(2,1)S(1)} %get-tuple-element.22), channel_id=1, source_target_pairs={{0,20},{4,24},{8,28},{12,0},{16,4},{20,8},{24,12},{28,16},{1,21},{... | collective-permute-start | bytes 448520 | tf_op jit(solution)/shard_map/ppermute | solution.py:262
  66.5 23.0 %collective-permute-start.5 = (bf16[584,128]{1,0:T(8,128)(2,1)S(1)}, bf16[584,128]{1,0:T(8,128)(2,1)S(1)}, u32[]{:S(2)}, u32[]{:S(2)}) collective-permute-start(bf16[584,128]{1,0:T(8,128)(2,1)S(1)} %get-tuple-element.23), channel_id=1, source_target_pairs={{0,24},{4,28},{8,0},{12,4},{16,8},{20,12},{24,16},{28,20},{1,25},{... | collective-permute-start | bytes 448520 | tf_op jit(solution)/shard_map/ppermute | solution.py:262
  72.4 17.1 %collective-permute-start.6 = (bf16[584,128]{1,0:T(8,128)(2,1)S(1)}, bf16[584,128]{1,0:T(8,128)(2,1)S(1)}, u32[]{:S(2)}, u32[]{:S(2)}) collective-permute-start(bf16[584,128]{1,0:T(8,128)(2,1)S(1)} %get-tuple-element.24), channel_id=1, source_target_pairs={{0,28},{4,0},{8,4},{12,8},{16,12},{20,16},{24,20},{28,24},{1,29},{... | collective-permute-start | bytes 448520 | tf_op jit(solution)/shard_map/ppermute | solution.py:262
  90.4 40.3 %collective-permute-start.7 = (bf16[8,144,128]{2,1,0:T(8,128)(2,1)}, bf16[8,144,128]{2,1,0:T(8,128)(2,1)S(1)}, u32[]{:S(2)}, u32[]{:S(2)}) collective-permute-start(bf16[8,144,128]{2,1,0:T(8,128)(2,1)} %get-tuple-element.26), channel_id=1, source_target_pairs={{0,1},{1,2},{2,3},{3,0},{4,5},{5,6},{6,7},{7,4},{8,9},{9,10},{10,1... | collective-permute-start | bytes 884744 | tf_op jit(solution)/shard_map/ppermute | solution.py:262
  91.7 39.0 %collective-permute-start.8 = (bf16[8,144,128]{2,1,0:T(8,128)(2,1)}, bf16[8,144,128]{2,1,0:T(8,128)(2,1)S(1)}, u32[]{:S(2)}, u32[]{:S(2)}) collective-permute-start(bf16[8,144,128]{2,1,0:T(8,128)(2,1)} %get-tuple-element.27), channel_id=1, source_target_pairs={{0,2},{1,3},{2,0},{3,1},{4,6},{5,7},{6,4},{7,5},{8,10},{9,11},{10,... | collective-permute-start | bytes 884744 | tf_op jit(solution)/shard_map/ppermute | solution.py:262
  94.7 36.0 %collective-permute-start.9 = (bf16[8,144,128]{2,1,0:T(8,128)(2,1)S(1)}, bf16[8,144,128]{2,1,0:T(8,128)(2,1)S(1)}, u32[]{:S(2)}, u32[]{:S(2)}) collective-permute-start(bf16[8,144,128]{2,1,0:T(8,128)(2,1)S(1)} %get-tuple-element.28), channel_id=1, source_target_pairs={{0,3},{1,0},{2,1},{3,2},{4,7},{5,4},{6,5},{7,6},{8,11},{9,8},{10,9... | collective-permute-start | bytes 884744 | tf_op jit(solution)/shard_map/ppermute | solution.py:262
  95.9 11.6 %collective-permute-start.12 = (bf16[8,8,128]{2,1,0:T(8,128)(2,1)S(1)}, bf16[8,8,128]{2,1,0:T(8,128)(2,1)S(1)}, u32[]{:S(2)}, u32[]{:S(2)}) collective-permute-start(bf16[8,8,128]{2,1,0:T(8,128)(2,1)S(1)} %router_tiles.1.refs_0_), channel_id=1, source_target_pairs={{0,3},{1,0},{2,1},{3,2},{4,7},{5,4},{6,5},{7,6},{8,11},{9,8},{10,9... | collective-permute-start | bytes 49160 | tf_op jit(solution)/shard_map/ppermute | solution.py:262
  96.0 12.7 %collective-permute-start.11 = (bf16[8,8,128]{2,1,0:T(8,128)(2,1)S(1)}, bf16[8,8,128]{2,1,0:T(8,128)(2,1)S(1)}, u32[]{:S(2)}, u32[]{:S(2)}) collective-permute-start(bf16[8,8,128]{2,1,0:T(8,128)(2,1)S(1)} %router_tiles.1.refs_0_), channel_id=1, source_target_pairs={{0,2},{1,3},{2,0},{3,1},{4,6},{5,7},{6,4},{7,5},{8,10},{9,11},{10,... | collective-permute-start | bytes 49160 | tf_op jit(solution)/shard_map/ppermute | solution.py:262
  107.5 4.7 %collective-permute-start.10 = (bf16[8,8,128]{2,1,0:T(8,128)(2,1)S(1)}, bf16[8,8,128]{2,1,0:T(8,128)(2,1)S(1)}, u32[]{:S(2)}, u32[]{:S(2)}) collective-permute-start(bf16[8,8,128]{2,1,0:T(8,128)(2,1)S(1)} %router_tiles.1.refs_0_), channel_id=1, source_target_pairs={{0,1},{1,2},{2,3},{3,0},{4,5},{5,6},{6,7},{7,4},{8,9},{9,10},{10,1... | collective-permute-start | bytes 49160 | tf_op jit(solution)/shard_map/ppermute | solution.py:262
where the time goes:
time: 138 us; the launch traced here: 137 us
  waiting for transfers between devices  65.6 us (48%)
  starting transfers between devices  35.4 us (26%)
  blocking collectives  16.3 us (12%)
  Pallas kernels  15.5 us (11%)
  local copies, waits for them, and re-layouts  3.92 us (3%)
    ppermute x13, waiting for transfers between devices, shifted(): lax.ppermute(block, axis, [(k, (k + by) % size) for k in range(size)])  65.6 us
    ppermute x13, starting transfers between devices, shifted(): lax.ppermute(block, axis, [(k, (k + by) % size) for k in range(size)])  23.3 us
    all_gather x1, blocking collectives, per_device(): everyone = lax.all_gather(router_rows(tiles), EXPERT, axis=0, tiled=True)  16.3 us
    all_to_all x1, starting transfers between devices, per_device(): got_rest = lax.all_to_all(rest, SHARD, 0, 0, tiled=True)  12 us
    pallas_call x1, Pallas kernels, unpack_rest(): pl.pallas_call(functools.partial(unpack_rest_kernel, left, own), grid=(le...  4.15 us
    pallas_call x1, Pallas kernels, pack_rest(): pl.pallas_call(functools.partial(pack_rest_kernel, left, shards, own), gr...  3.96 us
    unnamed x3, local copies, waits for them, and re-layouts  3.92 us
    pallas_call x1, Pallas kernels, pack_ringed(): pl.pallas_call(functools.partial(pack_ringed_kernel, zs, ys, own), grid=(...  3.73 us
  transfers between devices with their start and end apart: 14, of which 6 were waited for; matrix products, arithmetic and copies ran while one was open for 1% of the time, Pallas kernels for 5%

commit v1 on v0

v1 whole, which is shorter than its diff:
```python
import functools

import jax
import jax.numpy as jnp
from jax import lax
from jax.experimental import pallas as pl
from jax.experimental.pallas import tpu as pltpu
from jax.sharding import Mesh
from jax.sharding import PartitionSpec as P

EXPERT = ("x", "core")
SHARD = ("z", "y")
RINGED = 7
LANES = 128
TILE = 8

VMEM = pl.BlockSpec(memory_space=pltpu.VMEM)
HBM = pl.BlockSpec(memory_space=pl.ANY)
GRANT = pltpu.CompilerParams(vmem_limit_bytes=16 * 2**20)
RING = (4, 3, 5, 2, 6, 1, 7)
LATER = (0,) + RING[1:]
SIDES = (1, 3, 2)


def cost(size):
    return pl.CostEstimate(flops=10**8, bytes_accessed=size, transcendentals=0)


def packed(rows):
    return jax.ShapeDtypeStruct(rows, jnp.bfloat16)


def two_experts(unit_ref):
    swap = lax.axis_index("y") % 2
    stacked = jnp.concatenate([unit_ref[swap], unit_ref[1 - swap]], axis=0)
    return stacked.astype(jnp.bfloat16).T


def merged_pairs(first, second):
    low = lax.broadcasted_iota(jnp.int32, first.shape, first.ndim - 1) < LANES // 2
    here = jnp.where(low, first, second)
    there = jnp.where(low, second, first)
    return here, jnp.concatenate([there[..., LANES // 2 :], there[..., : LANES // 2]], axis=-1)


def fetched(sources, units_ref, sems):
    copies = [pltpu.make_async_copy(source, units_ref.at[n], sems.at[n]) for n, source in enumerate(sources)]
    for copy in copies:
        copy.start()
    for n, copy in enumerate(copies):
        copy.wait()
        yield n, two_experts(units_ref.at[n])


def router_tile(weight_ref, gain_ref):
    part = (weight_ref[...] * gain_ref[...]).astype(jnp.bfloat16)
    return jnp.concatenate([part[:TILE], part[TILE:]], axis=1)


def pack_first_kernel(zs, ys, own, master_ref, weight_ref, gain_ref, out_ref, units_ref, rows_ref, sems):
    out_ref[-TILE:, :] = router_tile(weight_ref, gain_ref)
    width = units_ref.shape[-1]
    first = lax.rem(lax.axis_index("z") + RING[0], zs) * (ys * own)
    base = jnp.minimum(first // LANES * LANES, zs * ys * own - width)
    columns = pl.ds(pl.multiple_of(base, LANES), width)
    for e, rows in fetched([master_ref.at[:, e, :, columns] for e in range(RINGED)], units_ref, sems):
        rows_ref[e % 2] = rows
        moved = rows_ref[e % 2, pl.ds(pl.multiple_of(first - base, TILE), ys * own), :]
        for y in range(ys):
            row = (y * RINGED + e) * own
            out_ref[row : row + own, :] = moved[y * own : (y + 1) * own]


def pack_ringed_kernel(zs, ys, own, master_ref, weight_ref, gain_ref, *refs):
    outs, (units_ref, rows_ref, sems) = refs[:-3], refs[-3:]
    z = lax.axis_index("z")
    tile = router_tile(weight_ref, gain_ref)
    for out in outs:
        out[-TILE:, :] = tile
    for e, rows in fetched([master_ref.at[:, e] for e in range(RINGED)], units_ref, sems):
        rows_ref[e % 2] = rows
        for dz, out in zip(LATER, outs):
            start = lax.rem(z + dz, zs) * (ys * own)
            moved = rows_ref[e % 2, pl.ds(pl.multiple_of(start, TILE), ys * own), :]
            for y in range(ys):
                row = (y * RINGED + e) * own
                out[row : row + own, :] = moved[y * own : (y + 1) * own]


def pack_for(kernel, outs, width, master, weight, gain, zs, ys):
    _, _, depth, wide = master.shape
    own = wide // (zs * ys)
    return pl.pallas_call(
        functools.partial(kernel, zs, ys, own),
        in_specs=[HBM, VMEM, VMEM],
        out_specs=[VMEM] * outs,
        out_shape=[packed((ys * RINGED * own + TILE, LANES))] * outs,
        scratch_shapes=[
            pltpu.VMEM((RINGED, 2, depth, width), jnp.float32),
            pltpu.VMEM((2, width, LANES), jnp.bfloat16),
            pltpu.SemaphoreType.DMA((RINGED,)),
        ],
        compiler_params=GRANT,
        cost_estimate=cost(4 * master.size),
    )(master, weight, gain)


def pack_ring(master, weight, gain, zs, ys):
    wide = master.shape[-1]
    width = -(-(wide // zs + LANES - TILE) // LANES) * LANES
    (first,) = pack_for(pack_first_kernel, 1, width, master, weight, gain, zs, ys)
    later = pack_for(pack_ringed_kernel, len(LATER), wide, master, weight, gain, zs, ys)
    near = dict(zip(LATER, later))
    near[RING[0]] = first
    return [near[dz] for dz in range(zs)]


def router_tiles_kernel(*refs):
    zs = len(refs) - 1
    z = lax.axis_index("z")
    for j in range(zs):
        refs[zs][lax.rem(z + zs - j, zs)] = refs[j][-TILE:, :]


def router_tiles(near):
    return pl.pallas_call(
        router_tiles_kernel,
        in_specs=[pl.BlockSpec((TILE, LANES), lambda e: (near[0].shape[0] // TILE - 1, 0))] * len(near),
        out_specs=VMEM,
        out_shape=packed((len(near), TILE, LANES)),
        grid=(1,),
        compiler_params=GRANT,
        name="router_tiles",
    )(*near)


def regroup_kernel(ys, *refs):
    zs = len(refs) - ys
    z, y = lax.axis_index("z"), lax.axis_index("y")
    rows = (refs[0].shape[0] - TILE) // ys
    for k in range(ys):
        start = pl.multiple_of(lax.rem(y + k, ys) * rows, TILE)
        for j in range(zs):
            refs[zs + k][lax.rem(z + zs - j, zs)] = refs[j][pl.ds(start, rows), :]


def regroup(near, ys):
    rows, lanes = near[0].shape
    shape = jax.ShapeDtypeStruct((len(near), (rows - TILE) // ys, lanes), jnp.bfloat16)
    return pl.pallas_call(
        functools.partial(regroup_kernel, ys),
        in_specs=[VMEM] * len(near),
        out_specs=[VMEM] * ys,
        out_shape=[shape] * ys,
        compiler_params=GRANT,
        name="regroup",
    )(*near)


def router_rows_kernel(*refs):
    out_ref = refs[-1]
    ys = len(refs) - 1
    y = lax.axis_index("y")

    def write(me):
        for even in range(0, ys, 2):
            a, b = (me - even) % ys, (me - even - 1) % ys
            for z in range(refs[0].shape[0]):
                first, second = refs[a][z], refs[b][z]
                column = (z * ys + even) * (LANES // 2)
                out_ref[:TILE, column : column + LANES] = jnp.concatenate(
                    [first[:, : LANES // 2], second[:, : LANES // 2]], axis=1
                )
                out_ref[TILE:, column : column + LANES] = jnp.concatenate(
                    [first[:, LANES // 2 :], second[:, LANES // 2 :]], axis=1
                )

    for me in range(ys):
        pl.when(y == me)(functools.partial(write, me))


def router_rows(tiles):
    zs, ys = tiles[0].shape[0], len(tiles)
    return pl.pallas_call(
        router_rows_kernel,
        in_specs=[VMEM] * ys,
        out_specs=VMEM,
        out_shape=packed((2 * TILE, zs * ys * LANES // 2)),
        compiler_params=GRANT,
        name="router_rows",
    )(*tiles)


def sent(targets, units_ref, sems, own, write):
    copies = []
    for n, target in enumerate(targets):
        write(units_ref.at[n], slice(n * own, (n + 1) * own))
        copies.append(pltpu.make_async_copy(units_ref.at[n], target, sems.at[n]))
        copies[-1].start()
    for copy in copies:
        copy.wait()


def unpack_ringed_kernel(own, *refs):
    groups, (out_ref, ordered_ref, units_ref, sems) = refs[:-4], refs[-4:]
    ys, zs = ordered_ref.shape[:2]
    y = lax.axis_index("y")
    for k, group in enumerate(groups):
        ordered_ref[lax.rem(y + ys - k, ys)] = group[...]

    def write(unit_ref, rows):
        for z in range(zs):
            for even in range(0, ys, 2):
                column = (z * ys + even) * (LANES // 2)
                here, there = merged_pairs(ordered_ref[even, z, rows, :], ordered_ref[even + 1, z, rows, :])
                unit_ref[0, :, column : column + LANES] = here
                unit_ref[1, :, column : column + LANES] = there

    sent([out_ref.at[:, e] for e in range(RINGED)], units_ref, sems, own, write)


def unpack_ringed(groups, half, own):
    zs, ys = groups[0].shape[0], len(groups)
    depth = zs * ys * LANES // 2
    return pl.pallas_call(
        functools.partial(unpack_ringed_kernel, own),
        in_specs=[VMEM] * ys,
        out_specs=HBM,
        out_shape=pltpu.HBM((2, half, own, depth), jnp.bfloat16),
        scratch_shapes=[
            pltpu.VMEM((ys, *groups[0].shape), jnp.bfloat16),
            pltpu.VMEM((RINGED, 2, own, depth), jnp.bfloat16),
            pltpu.SemaphoreType.DMA((RINGED,)),
        ],
        compiler_params=GRANT,
        cost_estimate=cost(8 * half * own * depth),
        name="unpack_ringed",
    )(*groups)


def rest_of(gate_ref, up_ref, half):
    return [gate_ref.at[:, e] for e in range(RINGED, half)] + [up_ref.at[:, e] for e in range(half)]


def pack_rest_kernel(shards, own, gate_ref, up_ref, out_ref, units_ref, rows_ref, sems, out_sems):
    copies = []
    for n, moved in fetched(rest_of(gate_ref, up_ref, gate_ref.shape[1]), units_ref, sems):
        rows = slice(n * own, (n + 1) * own)
        rows_ref[:, rows, :] = moved.reshape(shards, own, LANES)
        copies.append(pltpu.make_async_copy(rows_ref.at[:, rows], out_ref.at[:, rows], out_sems.at[n]))
        copies[-1].start()
    for copy in copies:
        copy.wait()


def pack_rest(gate, up, shards):
    _, half, depth, wide = gate.shape
    own, count = wide // shards, 2 * half - RINGED
    shape = (shards, count * own, LANES)
    return pl.pallas_call(
        functools.partial(pack_rest_kernel, shards, own),
        in_specs=[HBM] * 2,
        out_specs=HBM,
        out_shape=pltpu.HBM(shape, jnp.bfloat16),
        scratch_shapes=[
            pltpu.VMEM((count, 2, depth, wide), jnp.float32),
            pltpu.VMEM(shape, jnp.bfloat16),
            pltpu.SemaphoreType.DMA((count,)),
            pltpu.SemaphoreType.DMA((count,)),
        ],
        compiler_params=GRANT,
        cost_estimate=cost(8 * gate.size),
        name="pack_rest",
    )(gate, up)


def unpack_rest_kernel(own, in_ref, _, gate_ref, up_ref, units_ref, sems):
    def write(unit_ref, rows):
        for k in range(in_ref.shape[0] // 2):
            here, there = merged_pairs(in_ref[2 * k, rows, :], in_ref[2 * k + 1, rows, :])
            unit_ref[0, :, k * LANES : (k + 1) * LANES] = here
            unit_ref[1, :, k * LANES : (k + 1) * LANES] = there

    sent(rest_of(gate_ref, up_ref, gate_ref.shape[1]), units_ref, sems, own, write)


def unpack_rest(received, gate):
    _, half, own, depth = gate.shape
    count = 2 * half - RINGED
    return pl.pallas_call(
        functools.partial(unpack_rest_kernel, own),
        in_specs=[VMEM, HBM],
        out_specs=[HBM] * 2,
        out_shape=[pltpu.HBM(gate.shape, jnp.bfloat16)] * 2,
        scratch_shapes=[
            pltpu.VMEM((count, 2, own, depth), jnp.bfloat16),
            pltpu.SemaphoreType.DMA((count,)),
        ],
        input_output_aliases={1: 0},
        compiler_params=GRANT,
        cost_estimate=cost(8 * gate.size),
        name="unpack_rest",
    )(received, gate)


def in_hbm(array):
    return pltpu.with_memory_space_constraint(array, pltpu.HBM)


def shifted(block, axis, by):
    size = lax.axis_size(axis)
    return lax.ppermute(block, axis, [(k, (k + by) % size) for k in range(size)])


def per_device(master_gate, master_up, router_weight, router_gain):
    zs, ys = lax.axis_size("z"), lax.axis_size("y")
    experts, depth, wide = master_gate.shape
    half, own = experts // 2, wide // (zs * ys)
    gate, up = (m.reshape(2, half, depth, wide) for m in (master_gate, master_up))
    gate, up = in_hbm(gate), in_hbm(up)
    weight, gain = in_hbm(router_weight.T), in_hbm(router_gain[None])
    near = pack_ring(gate, weight, gain, zs, ys)
    for dz in RING:
        near[dz] = shifted(near[dz], "z", dz)
    rest = pack_rest(gate, up, zs * ys)
    got_rest = lax.all_to_all(rest, SHARD, 0, 0, tiled=True)
    tiles = [router_tiles(near)] * ys
    for dy in SIDES:
        tiles[dy] = shifted(tiles[dy], "y", dy)
    groups = list(regroup(near, ys))
    for dy in SIDES:
        groups[dy] = shifted(groups[dy], "y", dy)
    everyone = lax.all_gather(router_rows(tiles), EXPERT, axis=0, tiled=True)
    serve_router = everyone.T
    final_gate = unpack_ringed(groups, half, own)
    final_gate, final_up = unpack_rest(got_rest, final_gate)
    whole = (experts, own, zs * ys * depth)
    return final_gate.reshape(whole), final_up.reshape(whole), serve_router


def solution(mesh):
    torus = Mesh(mesh.devices.reshape(4, 2, 8, 4), ("x", "core", "z", "y"))
    return jax.shard_map(
        per_device,
        mesh=torus,
        in_specs=(P(EXPERT, SHARD, None), P(EXPERT, SHARD, None), P(SHARD, EXPERT), P(SHARD)),
        out_specs=(P(EXPERT, SHARD, None), P(EXPERT, SHARD, None), P()),
        check_vma=False,
    )
```

time: 138 us -> 134 us (0.971)
  Pallas kernels: 15.5 us -> 11.9 us
  local copies, waits for them, and re-layouts: 3.92 us -> 2.04 us
    pallas_call x5 -> x6, Pallas kernels: 14.4 us -> 10.8 us  [the longest x2 4.89 us: pack_for(): pl.pallas_call(functools.partial(kernel, zs, ys, own), in_specs=[HBM, VME...]
    unnamed x3 -> x1, local copies, waits for them, and re-layouts: 3.92 us -> 2.04 us
  transfers between devices with their start and end apart: 14 -> 14, of which waited for: 6 -> 6; matrix products, arithmetic and copies ran while one was open for 1% -> 2% of each run, Pallas kernels for 5% -> 6%
where the time goes in v1:
time: 134 us
  waiting for transfers between devices  66.7 us (50%)
  starting transfers between devices  36.2 us (27%)
  blocking collectives  16.3 us (12%)
  Pallas kernels  11.9 us (9%)
  local copies, waits for them, and re-layouts  2.04 us (2%)
    ppermute x13, waiting for transfers between devices, shifted(): lax.ppermute(block, axis, [(k, (k + by) % size) for k in range(size)])  66.7 us
    ppermute x13, starting transfers between devices, shifted(): lax.ppermute(block, axis, [(k, (k + by) % size) for k in range(size)])  24.1 us
    all_gather x1, blocking collectives, per_device(): everyone = lax.all_gather(router_rows(tiles), EXPERT, axis=0, tiled=True)  16.3 us
    all_to_all x1, starting transfers between devices, per_device(): got_rest = lax.all_to_all(rest, SHARD, 0, 0, tiled=True)  12 us
    pallas_call x2, Pallas kernels, pack_for(): pl.pallas_call(functools.partial(kernel, zs, ys, own), in_specs=[HBM, VME...  4.89 us
    pallas_call x1, Pallas kernels, pack_rest(): pl.pallas_call(functools.partial(pack_rest_kernel, shards, own), in_specs...  2.91 us
  transfers between devices with their start and end apart: 14, of which 6 were waited for; matrix products, arithmetic and copies ran while one was open for 2% of the time, Pallas kernels for 6%

profile of v1, /device:TPU:1, one launch (start us, length us, event | category | flops | bytes accessed | tf_op | source)
XLA Modules:
  0.0 133.9 jit_solution(4800961391276904817)
XLA Ops:
  0.6 2.9 %pack_rest.1 = bf16[32,216,128]{2,1,0:T(8,128)(2,1)} custom-call(f32[2,8,64,768]{3,2,1,0:T(8,128)} %bitcast.7, f32[2,8,64,768]{3,2,1,0:T(8,128)} %bitcast.11), custom_call_target="tpu_custom_call" | custom-call | flops 100000000 | bytes 6291456 | tf_op jit(solution)/shard_map/pack_rest/pallas_call | solution.py:260
  3.5 12.0 %all-to-all-start = ((bf16[32,216,128]{2,1,0:T(8,128)(2,1)}), bf16[32,216,128]{2,1,0:T(8,128)(2,1)S(1)}, u32[]{:S(2)}, u32[]{:S(2)}) async-start(bf16[32,216,128]{2,1,0:T(8,128)(2,1)} %pack_rest.1), calls=%async_computation | async-start | bytes 3538944 | tf_op jit(solution)/shard_map/all_to_all | solution.py:326
  15.6 2.3 %shard_map.68 = bf16[680,128]{1,0:T(8,128)(2,1)S(1)} custom-call(f32[2,8,64,768]{3,2,1,0:T(8,128)} %bitcast.8, f32[16,64]{1,0:T(8,128)} %bitcast.13, f32[1,64]{1,0:T(1,128)} %bitcast.15), custom_call_target="tpu_custom_call" | custom-call | flops 100000000 | bytes 3145728 | tf_op jit(solution)/shard_map/pallas_call | solution.py:93
  17.9 5.2 %collective-permute-start.3 = (bf16[680,128]{1,0:T(8,128)(2,1)S(1)}, bf16[680,128]{1,0:T(8,128)(2,1)S(1)}, u32[]{:S(2)}, u32[]{:S(2)}) collective-permute-start(bf16[680,128]{1,0:T(8,128)(2,1)S(1)} %shard_map.68), channel_id=1, source_target_pairs={{0,16},{4,20},{8,24},{12,28},{16,0},{20,4},{24,8},{28,12},{1,17},{... | collective-permute-start | bytes 522248 | tf_op jit(solution)/shard_map/ppermute | solution.py:312
  23.1 2.6 %shard_map.67 = (bf16[680,128]{1,0:T(8,128)(2,1)S(1)}, bf16[680,128]{1,0:T(8,128)(2,1)S(1)}, bf16[680,128]{1,0:T(8,128)(2,1)S(1)}, bf16[680,128]{1,0:T(8,128)(2,...) custom-call(f32[2,8,64,768]{3,2,1,0:T(8,128)} %bitcast.9, ...), custom_call_target="tpu_custom_call" | custom-call | flops 100000000 | bytes 3145728 | tf_op jit(solution)/shard_map/pallas_call | solution.py:93
  26.5 2.0 %collective-permute-start.2 = (bf16[680,128]{1,0:T(8,128)(2,1)S(1)}, bf16[680,128]{1,0:T(8,128)(2,1)S(1)}, u32[]{:S(2)}, u32[]{:S(2)}) collective-permute-start(bf16[680,128]{1,0:T(8,128)(2,1)S(1)} %get-tuple-element.19), channel_id=1, source_target_pairs={{0,12},{4,16},{8,20},{12,24},{16,28},{20,0},{24,4},{28,8},{1,13},{... | collective-permute-start | bytes 522248 | tf_op jit(solution)/shard_map/ppermute | solution.py:312
  28.5 2.4 %collective-permute-start.4 = (bf16[680,128]{1,0:T(8,128)(2,1)S(1)}, bf16[680,128]{1,0:T(8,128)(2,1)S(1)}, u32[]{:S(2)}, u32[]{:S(2)}) collective-permute-start(bf16[680,128]{1,0:T(8,128)(2,1)S(1)} %get-tuple-element.20), channel_id=1, source_target_pairs={{0,20},{4,24},{8,28},{12,0},{16,4},{20,8},{24,12},{28,16},{1,21},{... | collective-permute-start | bytes 522248 | tf_op jit(solution)/shard_map/ppermute | solution.py:312
  31.0 32.1 %collective-permute-done.3.refs_4_ = bf16[680,128]{1,0:T(8,128)(2,1)S(1)} collective-permute-done((bf16[680,128]{1,0:T(8,128)(2,1)S(1)}, bf16[680,128]{1,0:T(8,128)(2,1)S(1)}, u32[]{:S(2)}, u32[]{:S(2)}) %collective-permute-start.3) | collective-permute-done | bytes 174112 | tf_op jit(solution)/shard_map/ppermute | solution.py:312
  63.0 4.0 %collective-permute-start.5 = (bf16[680,128]{1,0:T(8,128)(2,1)S(1)}, bf16[680,128]{1,0:T(8,128)(2,1)S(1)}, u32[]{:S(2)}, u32[]{:S(2)}) collective-permute-start(bf16[680,128]{1,0:T(8,128)(2,1)S(1)} %get-tuple-element.21), channel_id=1, source_target_pairs={{0,24},{4,28},{8,0},{12,4},{16,8},{20,12},{24,16},{28,20},{1,25},{... | collective-permute-start | bytes 522248 | tf_op jit(solution)/shard_map/ppermute | solution.py:312
  67.4 1.3 collective-permute-start.6
  68.7 5.0 %collective-permute-done.1.refs_2_ = bf16[680,128]{1,0:T(8,128)(2,1)S(1)} collective-permute-done((bf16[680,128]{1,0:T(8,128)(2,1)S(1)}, bf16[680,128]{1,0:T(8,128)(2,1)S(1)}, u32[]{:S(2)}, u32[]{:S(2)}) %collective-permute-start.1) | collective-permute-done | bytes 174112 | tf_op jit(solution)/shard_map/ppermute | solution.py:312
  73.8 14.2 %collective-permute-done.2.refs_3_ = bf16[680,128]{1,0:T(8,128)(2,1)S(1)} collective-permute-done((bf16[680,128]{1,0:T(8,128)(2,1)S(1)}, bf16[680,128]{1,0:T(8,128)(2,1)S(1)}, u32[]{:S(2)}, u32[]{:S(2)}) %collective-permute-start.2) | collective-permute-done | bytes 174112 | tf_op jit(solution)/shard_map/ppermute | solution.py:312
  88.0 1.0 regroup.1
  88.9 1.2 collective-permute-start.7
  90.1 2.4 %collective-permute-start.8 = (bf16[8,168,128]{2,1,0:T(8,128)(2,1)}, bf16[8,168,128]{2,1,0:T(8,128)(2,1)S(1)}, u32[]{:S(2)}, u32[]{:S(2)}) collective-permute-start(bf16[8,168,128]{2,1,0:T(8,128)(2,1)} %get-tuple-element.25), channel_id=1, source_target_pairs={{0,2},{1,3},{2,0},{3,1},{4,6},{5,7},{6,4},{7,5},{8,10},{9,11},{10,... | collective-permute-start | bytes 1032200 | tf_op jit(solution)/shard_map/ppermute | solution.py:312
  92.6 1.2 collective-permute-start.9
  93.8 2.1 %collective-permute-start.11 = (bf16[8,8,128]{2,1,0:T(8,128)(2,1)S(1)}, bf16[8,8,128]{2,1,0:T(8,128)(2,1)S(1)}, u32[]{:S(2)}, u32[]{:S(2)}) collective-permute-start(bf16[8,8,128]{2,1,0:T(8,128)(2,1)S(1)} %router_tiles.1.refs_0_), channel_id=1, source_target_pairs={{0,2},{1,3},{2,0},{3,1},{4,6},{5,7},{6,4},{7,5},{8,10},{9,11},{10,... | collective-permute-start | bytes 49160 | tf_op jit(solution)/shard_map/ppermute | solution.py:312
  95.9 11.9 %collective-permute-done.12.refs_3_ = bf16[8,8,128]{2,1,0:T(8,128)(2,1)S(1)} collective-permute-done((bf16[8,8,128]{2,1,0:T(8,128)(2,1)S(1)}, bf16[8,8,128]{2,1,0:T(8,128)(2,1)S(1)}, u32[]{:S(2)}, u32[]{:S(2)}) %collective-permute-start.12) | collective-permute-done | bytes 16416 | tf_op jit(solution)/shard_map/ppermute | solution.py:312
  107.8 1.4 %collective-permute-start.10 = (bf16[8,8,128]{2,1,0:T(8,128)(2,1)S(1)}, bf16[8,8,128]{2,1,0:T(8,128)(2,1)S(1)}, u32[]{:S(2)}, u32[]{:S(2)}) collective-permute-start(bf16[8,8,128]{2,1,0:T(8,128)(2,1)S(1)} %router_tiles.1.refs_0_), channel_id=1, source_target_pairs={{0,1},{1,2},{2,3},{3,0},{4,5},{5,6},{6,7},{7,4},{8,9},{9,10},{10,1... | collective-permute-start | bytes 49160 | tf_op jit(solution)/shard_map/ppermute | solution.py:312
  109.2 3.1 %collective-permute-done.10.refs_1_ = bf16[8,8,128]{2,1,0:T(8,128)(2,1)S(1)} collective-permute-done((bf16[8,8,128]{2,1,0:T(8,128)(2,1)S(1)}, bf16[8,8,128]{2,1,0:T(8,128)(2,1)S(1)}, u32[]{:S(2)}, u32[]{:S(2)}) %collective-permute-start.10) | collective-permute-done | bytes 16416 | tf_op jit(solution)/shard_map/ppermute | solution.py:312
  112.5 16.3 %all_gather.3 = bf16[128,2048]{1,0:T(8,128)(2,1)} all-gather(bf16[16,2048]{1,0:T(8,128)(2,1)S(1)} %router_rows.1), channel_id=1, replica_groups=mesh['x'=4,'core'=2,'z'=8,'y'=4] {'x','core'}, dimensions={0}, use_global_device_ids=true | all-gather | bytes 589824 | tf_op jit(solution)/shard_map/all_gather | solution.py:333
  128.8 2.0 %copy.8 = bf16[2048,128]{1,0:T(8,128)(2,1)} copy(bf16[2048,128]{0,1:T(8,128)(2,1)} %bitcast.12) | data formatting | bytes 1048576
  130.9 1.6 %unpack_ringed.1._ = bf16[2,8,24,2048]{3,2,1,0:T(8,128)(2,1)} custom-call(bf16[8,168,128]{2,1,0:T(8,128)(2,1)S(1)} %get-tuple-element.23.refs_0_, bf16[8,168,128]{2,1,0:T(8,128)(2,1)S(1)} %collective-permute-done.7.refs_1_, bf16[8,168,128]{2,1,0:T(8,128)(2,1)S(1)} %collective-permute-done.8.refs_2_, bf16[8,168,128]{2,1,0:T(8,128)(2,1)S(1)} %collective-permute-done.9.refs_3_), custom_call_target="tpu_custom_call" | custom-call | flops 100000000 | bytes 3145728 | tf_op jit(solution)/shard_map/unpack_ringed/pallas_call | solution.py:225
  132.5 1.4 %unpack_rest.1 = (bf16[2,8,24,2048]{3,2,1,0:T(8,128)(2,1)}, bf16[2,8,24,2048]{3,2,1,0:T(8,128)(2,1)}) custom-call(bf16[32,216,128]{2,1,0:T(8,128)(2,1)S(1)} %all-to-all-done.in_ref, bf16[2,8,24,2048]{3,2,1,0:T(8,128)(2,1)} %unpack_ringed.1._), custom_call_target="tpu_custom_call", output_to_operand_aliasing={{0}: (1, {})} | custom-call | flops 100000000 | bytes 6291456 | tf_op jit(solution)/shard_map/unpack_rest/pallas_call | solution.py:290
  (14 shorter events, 1.4 us)
Async XLA Ops:
  3.5 128.9 %all-to-all-start = ((bf16[32,216,128]{2,1,0:T(8,128)(2,1)}), bf16[32,216,128]{2,1,0:T(8,128)(2,1)S(1)}, u32[]{:S(2)}, u32[]{:S(2)}) async-start(bf16[32,216,128]{2,1,0:T(8,128)(2,1)} %pack_rest.1), calls=%async_computation | async-start | bytes 3538944 | tf_op jit(solution)/shard_map/all_to_all | solution.py:326
  17.9 45.2 %collective-permute-start.3 = (bf16[680,128]{1,0:T(8,128)(2,1)S(1)}, bf16[680,128]{1,0:T(8,128)(2,1)S(1)}, u32[]{:S(2)}, u32[]{:S(2)}) collective-permute-start(bf16[680,128]{1,0:T(8,128)(2,1)S(1)} %shard_map.68), channel_id=1, source_target_pairs={{0,16},{4,20},{8,24},{12,28},{16,0},{20,4},{24,8},{28,12},{1,17},{... | collective-permute-start | bytes 522248 | tf_op jit(solution)/shard_map/ppermute | solution.py:312
  25.7 41.7 %collective-permute-start = (bf16[680,128]{1,0:T(8,128)(2,1)S(1)}, bf16[680,128]{1,0:T(8,128)(2,1)S(1)}, u32[]{:S(2)}, u32[]{:S(2)}) collective-permute-start(bf16[680,128]{1,0:T(8,128)(2,1)S(1)} %get-tuple-element.17), channel_id=1, source_target_pairs={{0,4},{4,8},{8,12},{12,16},{16,20},{20,24},{24,28},{28,0},{1,5},{5... | collective-permute-start | bytes 522248 | tf_op jit(solution)/shard_map/ppermute | solution.py:312
  26.1 47.6 %collective-permute-start.1 = (bf16[680,128]{1,0:T(8,128)(2,1)S(1)}, bf16[680,128]{1,0:T(8,128)(2,1)S(1)}, u32[]{:S(2)}, u32[]{:S(2)}) collective-permute-start(bf16[680,128]{1,0:T(8,128)(2,1)S(1)} %get-tuple-element.18), channel_id=1, source_target_pairs={{0,8},{4,12},{8,16},{12,20},{16,24},{20,28},{24,0},{28,4},{1,9},{5... | collective-permute-start | bytes 522248 | tf_op jit(solution)/shard_map/ppermute | solution.py:312
  26.5 61.5 %collective-permute-start.2 = (bf16[680,128]{1,0:T(8,128)(2,1)S(1)}, bf16[680,128]{1,0:T(8,128)(2,1)S(1)}, u32[]{:S(2)}, u32[]{:S(2)}) collective-permute-start(bf16[680,128]{1,0:T(8,128)(2,1)S(1)} %get-tuple-element.19), channel_id=1, source_target_pairs={{0,12},{4,16},{8,20},{12,24},{16,28},{20,0},{24,4},{28,8},{1,13},{... | collective-permute-start | bytes 522248 | tf_op jit(solution)/shard_map/ppermute | solution.py:312
  28.5 59.4 %collective-permute-start.4 = (bf16[680,128]{1,0:T(8,128)(2,1)S(1)}, bf16[680,128]{1,0:T(8,128)(2,1)S(1)}, u32[]{:S(2)}, u32[]{:S(2)}) collective-permute-start(bf16[680,128]{1,0:T(8,128)(2,1)S(1)} %get-tuple-element.20), channel_id=1, source_target_pairs={{0,20},{4,24},{8,28},{12,0},{16,4},{20,8},{24,12},{28,16},{1,21},{... | collective-permute-start | bytes 522248 | tf_op jit(solution)/shard_map/ppermute | solution.py:312
  63.0 24.9 %collective-permute-start.5 = (bf16[680,128]{1,0:T(8,128)(2,1)S(1)}, bf16[680,128]{1,0:T(8,128)(2,1)S(1)}, u32[]{:S(2)}, u32[]{:S(2)}) collective-permute-start(bf16[680,128]{1,0:T(8,128)(2,1)S(1)} %get-tuple-element.21), channel_id=1, source_target_pairs={{0,24},{4,28},{8,0},{12,4},{16,8},{20,12},{24,16},{28,20},{1,25},{... | collective-permute-start | bytes 522248 | tf_op jit(solution)/shard_map/ppermute | solution.py:312
  67.4 20.5 %collective-permute-start.6 = (bf16[680,128]{1,0:T(8,128)(2,1)S(1)}, bf16[680,128]{1,0:T(8,128)(2,1)S(1)}, u32[]{:S(2)}, u32[]{:S(2)}) collective-permute-start(bf16[680,128]{1,0:T(8,128)(2,1)S(1)} %get-tuple-element.22), channel_id=1, source_target_pairs={{0,28},{4,0},{8,4},{12,8},{16,12},{20,16},{24,20},{28,24},{1,29},{... | collective-permute-start | bytes 522248 | tf_op jit(solution)/shard_map/ppermute | solution.py:312
  88.9 41.9 %collective-permute-start.7 = (bf16[8,168,128]{2,1,0:T(8,128)(2,1)}, bf16[8,168,128]{2,1,0:T(8,128)(2,1)S(1)}, u32[]{:S(2)}, u32[]{:S(2)}) collective-permute-start(bf16[8,168,128]{2,1,0:T(8,128)(2,1)} %get-tuple-element.24), channel_id=1, source_target_pairs={{0,1},{1,2},{2,3},{3,0},{4,5},{5,6},{6,7},{7,4},{8,9},{9,10},{10,1... | collective-permute-start | bytes 1032200 | tf_op jit(solution)/shard_map/ppermute | solution.py:312
  90.1 40.7 %collective-permute-start.8 = (bf16[8,168,128]{2,1,0:T(8,128)(2,1)}, bf16[8,168,128]{2,1,0:T(8,128)(2,1)S(1)}, u32[]{:S(2)}, u32[]{:S(2)}) collective-permute-start(bf16[8,168,128]{2,1,0:T(8,128)(2,1)} %get-tuple-element.25), channel_id=1, source_target_pairs={{0,2},{1,3},{2,0},{3,1},{4,6},{5,7},{6,4},{7,5},{8,10},{9,11},{10,... | collective-permute-start | bytes 1032200 | tf_op jit(solution)/shard_map/ppermute | solution.py:312
  92.6 38.3 %collective-permute-start.9 = (bf16[8,168,128]{2,1,0:T(8,128)(2,1)S(1)}, bf16[8,168,128]{2,1,0:T(8,128)(2,1)S(1)}, u32[]{:S(2)}, u32[]{:S(2)}) collective-permute-start(bf16[8,168,128]{2,1,0:T(8,128)(2,1)S(1)} %get-tuple-element.26), channel_id=1, source_target_pairs={{0,3},{1,0},{2,1},{3,2},{4,7},{5,4},{6,5},{7,6},{8,11},{9,8},{10,9... | collective-permute-start | bytes 1032200 | tf_op jit(solution)/shard_map/ppermute | solution.py:312
  93.7 14.1 %collective-permute-start.12 = (bf16[8,8,128]{2,1,0:T(8,128)(2,1)S(1)}, bf16[8,8,128]{2,1,0:T(8,128)(2,1)S(1)}, u32[]{:S(2)}, u32[]{:S(2)}) collective-permute-start(bf16[8,8,128]{2,1,0:T(8,128)(2,1)S(1)} %router_tiles.1.refs_0_), channel_id=1, source_target_pairs={{0,3},{1,0},{2,1},{3,2},{4,7},{5,4},{6,5},{7,6},{8,11},{9,8},{10,9... | collective-permute-start | bytes 49160 | tf_op jit(solution)/shard_map/ppermute | solution.py:312
  93.8 15.4 %collective-permute-start.11 = (bf16[8,8,128]{2,1,0:T(8,128)(2,1)S(1)}, bf16[8,8,128]{2,1,0:T(8,128)(2,1)S(1)}, u32[]{:S(2)}, u32[]{:S(2)}) collective-permute-start(bf16[8,8,128]{2,1,0:T(8,128)(2,1)S(1)} %router_tiles.1.refs_0_), channel_id=1, source_target_pairs={{0,2},{1,3},{2,0},{3,1},{4,6},{5,7},{6,4},{7,5},{8,10},{9,11},{10,... | collective-permute-start | bytes 49160 | tf_op jit(solution)/shard_map/ppermute | solution.py:312
  107.8 4.5 %collective-permute-start.10 = (bf16[8,8,128]{2,1,0:T(8,128)(2,1)S(1)}, bf16[8,8,128]{2,1,0:T(8,128)(2,1)S(1)}, u32[]{:S(2)}, u32[]{:S(2)}) collective-permute-start(bf16[8,8,128]{2,1,0:T(8,128)(2,1)S(1)} %router_tiles.1.refs_0_), channel_id=1, source_target_pairs={{0,1},{1,2},{2,3},{3,0},{4,5},{5,6},{6,7},{7,4},{8,9},{9,10},{10,1... | collective-permute-start | bytes 49160 | tf_op jit(solution)/shard_map/ppermute | solution.py:312

commit v2 on v1

v2 whole, which is shorter than its diff:
```python
import functools

import jax
import jax.numpy as jnp
from jax import lax
from jax.experimental import pallas as pl
from jax.experimental.pallas import tpu as pltpu
from jax.sharding import Mesh
from jax.sharding import PartitionSpec as P

EXPERT = ("x", "core")
SHARD = ("z", "y")
LANES = 128
TILE = 8
CHUNK = 48

VMEM = pl.BlockSpec(memory_space=pltpu.VMEM)
HBM = pl.BlockSpec(memory_space=pl.ANY)
GRANT = pltpu.CompilerParams(vmem_limit_bytes=16 * 2**20)
RING = (4, 1, 7, 3, 5, 2, 6)
BATCHES = ((0, 4, 1, 7), (3, 5, 2, 6))
LATER = (0,) + RING[1:]
SIDES = (1, 3, 2)


def cost(size):
    return pl.CostEstimate(flops=10**8, bytes_accessed=size, transcendentals=0)


def packed(rows):
    return jax.ShapeDtypeStruct(rows, jnp.bfloat16)


def two_experts(unit_ref):
    swap = lax.axis_index("y") % 2
    stacked = jnp.concatenate([unit_ref[swap], unit_ref[1 - swap]], axis=0)
    return stacked.astype(jnp.bfloat16).T


def merged_pairs(first, second):
    low = lax.broadcasted_iota(jnp.int32, first.shape, first.ndim - 1) < LANES // 2
    here = jnp.where(low, first, second)
    there = jnp.where(low, second, first)
    return here, jnp.concatenate([there[..., LANES // 2 :], there[..., : LANES // 2]], axis=-1)


def fetched(sources, units_ref, sems, beside=None):
    copies = [pltpu.make_async_copy(source, units_ref.at[n], sems.at[n]) for n, source in enumerate(sources)]
    for copy in copies:
        copy.start()
    if beside is not None:
        next(beside)
    for n, copy in enumerate(copies):
        copy.wait()
        yield n, two_experts(units_ref.at[n])


def router_tile(router_refs, held_refs, sems):
    copies = [pltpu.make_async_copy(a, b, sems.at[n]) for n, (a, b) in enumerate(zip(router_refs, held_refs))]
    for copy in copies:
        copy.start()
    yield
    for copy in copies:
        copy.wait()
    part = (held_refs[0][...] * held_refs[1][...]).astype(jnp.bfloat16)
    yield jnp.concatenate([part[:TILE], part[TILE:]], axis=1)


def pack_first_kernel(zs, ys, own, master_ref, *refs):
    (out_ref,), (units_ref, rows_ref, sems, *held, held_sems) = refs[2:3], refs[3:]
    width = units_ref.shape[-1]
    first = lax.rem(lax.axis_index("z") + RING[0], zs) * (ys * own)
    base = jnp.minimum(first // LANES * LANES, zs * ys * own - width)
    columns = pl.ds(pl.multiple_of(base, LANES), width)
    sources = [master_ref.at[:, e, :, columns] for e in range(units_ref.shape[0])]
    tile = router_tile(refs[:2], held, held_sems)
    for e, rows in fetched(sources, units_ref, sems, tile):
        rows_ref[e % 2] = rows
        moved = rows_ref[e % 2, pl.ds(pl.multiple_of(first - base, TILE), ys * own), :]
        for y in range(ys):
            row = (y * units_ref.shape[0] + e) * own
            out_ref[row : row + own, :] = moved[y * own : (y + 1) * own]
    out_ref[-TILE:, :] = next(tile)


def pack_ringed_kernel(zs, ys, own, master_ref, *refs):
    outs, (units_ref, rows_ref, sems, *held, held_sems) = refs[2 : 2 + len(LATER)], refs[2 + len(LATER) :]
    z = lax.axis_index("z")
    tile = router_tile(refs[:2], held, held_sems)
    for e, rows in fetched([master_ref.at[:, e] for e in range(units_ref.shape[0])], units_ref, sems, tile):
        rows_ref[e % 2] = rows
        for dz, out in zip(LATER, outs):
            start = lax.rem(z + dz, zs) * (ys * own)
            moved = rows_ref[e % 2, pl.ds(pl.multiple_of(start, TILE), ys * own), :]
            for y in range(ys):
                row = (y * units_ref.shape[0] + e) * own
                out[row : row + own, :] = moved[y * own : (y + 1) * own]
    tile = next(tile)
    for out in outs:
        out[-TILE:, :] = tile


def pack_for(kernel, outs, width, master, weight, gain, zs, ys):
    _, half, depth, wide = master.shape
    own = wide // (zs * ys)
    return pl.pallas_call(
        functools.partial(kernel, zs, ys, own),
        in_specs=[HBM] * 3,
        out_specs=[VMEM] * outs,
        out_shape=[packed((ys * half * own + TILE, LANES))] * outs,
        scratch_shapes=[
            pltpu.VMEM((half, 2, depth, width), jnp.float32),
            pltpu.VMEM((2, width, LANES), jnp.bfloat16),
            pltpu.SemaphoreType.DMA((half,)),
            pltpu.VMEM(weight.shape, jnp.float32),
            pltpu.VMEM(gain.shape, jnp.float32),
            pltpu.SemaphoreType.DMA((2,)),
        ],
        compiler_params=GRANT,
        cost_estimate=cost(4 * master.size),
    )(master, weight, gain)


def pack_ring(master, weight, gain, zs, ys):
    wide = master.shape[-1]
    width = -(-(wide // zs + LANES - TILE) // LANES) * LANES
    (first,) = pack_for(pack_first_kernel, 1, width, master, weight, gain, zs, ys)
    later = pack_for(pack_ringed_kernel, len(LATER), wide, master, weight, gain, zs, ys)
    near = dict(zip(LATER, later))
    near[RING[0]] = first
    return [near[dz] for dz in range(zs)]


def router_tiles_kernel(*refs):
    zs = len(refs) - 1
    z = lax.axis_index("z")
    for j in range(zs):
        refs[zs][lax.rem(z + zs - j, zs)] = refs[j][-TILE:, :]


def router_tiles(near):
    return pl.pallas_call(
        router_tiles_kernel,
        in_specs=[pl.BlockSpec((TILE, LANES), lambda e: (near[0].shape[0] // TILE - 1, 0))] * len(near),
        out_specs=VMEM,
        out_shape=packed((len(near), TILE, LANES)),
        grid=(1,),
        compiler_params=GRANT,
        name="router_tiles",
    )(*near)


def regroup_kernel(ys, *refs):
    count = len(refs) - ys
    y = lax.axis_index("y")
    rows = refs[count].shape[1]
    for k in range(ys):
        start = pl.multiple_of(lax.rem(y + k, ys) * rows, TILE)
        for n in range(count):
            refs[count + k][n] = refs[n][pl.ds(start, rows), :]


def regroup(near, ys):
    rows, lanes = near[0].shape
    shape = packed((len(near), (rows - TILE) // ys, lanes))
    return pl.pallas_call(
        functools.partial(regroup_kernel, ys),
        in_specs=[VMEM] * len(near),
        out_specs=[VMEM] * ys,
        out_shape=[shape] * ys,
        compiler_params=GRANT,
    )(*near)


def router_rows_kernel(*refs):
    out_ref = refs[-1]
    ys = len(refs) - 1
    y = lax.axis_index("y")

    def write(me):
        for even in range(0, ys, 2):
            a, b = (me - even) % ys, (me - even - 1) % ys
            for z in range(refs[0].shape[0]):
                first, second = refs[a][z], refs[b][z]
                column = (z * ys + even) * (LANES // 2)
                out_ref[:TILE, column : column + LANES] = jnp.concatenate(
                    [first[:, : LANES // 2], second[:, : LANES // 2]], axis=1
                )
                out_ref[TILE:, column : column + LANES] = jnp.concatenate(
                    [first[:, LANES // 2 :], second[:, LANES // 2 :]], axis=1
                )

    for me in range(ys):
        pl.when(y == me)(functools.partial(write, me))


def router_rows(tiles):
    zs, ys = tiles[0].shape[0], len(tiles)
    return pl.pallas_call(
        router_rows_kernel,
        in_specs=[VMEM] * ys,
        out_specs=VMEM,
        out_shape=packed((2 * TILE, zs * ys * LANES // 2)),
        compiler_params=GRANT,
        name="router_rows",
    )(*tiles)


def sent(out_ref, units_ref, sems, write):
    count, _, rows, _ = units_ref.shape
    copies = []
    for n in range(count):
        part = slice(n * rows, (n + 1) * rows)
        write(units_ref.at[n], part)
        copies.append(pltpu.make_async_copy(units_ref.at[n], out_ref.at[:, part], sems.at[n]))
        copies[-1].start()
    for copy in copies:
        copy.wait()


def unpack(kernel, operands, scratch, rows, depth):
    return pl.pallas_call(
        kernel,
        in_specs=[VMEM] * len(operands),
        out_specs=HBM,
        out_shape=pltpu.HBM((2, rows, depth), jnp.bfloat16),
        scratch_shapes=[
            *scratch,
            pltpu.VMEM((rows // CHUNK, 2, CHUNK, depth), jnp.bfloat16),
            pltpu.SemaphoreType.DMA((rows // CHUNK,)),
        ],
        compiler_params=GRANT,
        cost_estimate=cost(8 * rows * depth),
    )(*operands)


def unpack_ringed_kernel(*refs):
    groups, (out_ref, ordered_ref, units_ref, sems) = refs[:-4], refs[-4:]
    ys, zs = ordered_ref.shape[:2]
    z, y = lax.axis_index("z"), lax.axis_index("y")
    for n, group in enumerate(groups):
        for place, dz in enumerate(BATCHES[n // ys]):
            ordered_ref[lax.rem(y + ys - n % ys, ys), lax.rem(z + zs - dz, zs)] = group[place]

    def write(unit_ref, part):
        for z in range(zs):
            for even in range(0, ys, 2):
                column = (z * ys + even) * (LANES // 2)
                here, there = merged_pairs(ordered_ref[even, z, part, :], ordered_ref[even + 1, z, part, :])
                unit_ref[0, :, column : column + LANES] = here
                unit_ref[1, :, column : column + LANES] = there

    sent(out_ref, units_ref, sems, write)


def unpack_rest_kernel(in_ref, out_ref, units_ref, sems):
    def write(unit_ref, part):
        for k in range(in_ref.shape[0] // 2):
            here, there = merged_pairs(in_ref[2 * k, part, :], in_ref[2 * k + 1, part, :])
            unit_ref[0, :, k * LANES : (k + 1) * LANES] = here
            unit_ref[1, :, k * LANES : (k + 1) * LANES] = there

    sent(out_ref, units_ref, sems, write)


def pack_rest_kernel(shards, own, up_ref, out_ref, units_ref, rows_ref, sems, out_sems):
    copies = []
    half = up_ref.shape[1]
    for n, moved in fetched([up_ref.at[:, e] for e in range(half)], units_ref, sems):
        rows = slice(n * own, (n + 1) * own)
        rows_ref[:, rows, :] = moved.reshape(shards, own, LANES)
        copies.append(pltpu.make_async_copy(rows_ref.at[:, rows], out_ref.at[:, rows], out_sems.at[n]))
        copies[-1].start()
    for copy in copies:
        copy.wait()


def pack_rest(up, shards):
    _, half, depth, wide = up.shape
    own = wide // shards
    shape = (shards, half * own, LANES)
    return pl.pallas_call(
        functools.partial(pack_rest_kernel, shards, own),
        in_specs=[HBM],
        out_specs=HBM,
        out_shape=pltpu.HBM(shape, jnp.bfloat16),
        scratch_shapes=[
            pltpu.VMEM((half, 2, depth, wide), jnp.float32),
            pltpu.VMEM(shape, jnp.bfloat16),
            pltpu.SemaphoreType.DMA((half,)),
            pltpu.SemaphoreType.DMA((half,)),
        ],
        compiler_params=GRANT,
        cost_estimate=cost(6 * up.size),
        name="pack_rest",
    )(up)


def in_hbm(array):
    return pltpu.with_memory_space_constraint(array, pltpu.HBM)


def shifted(block, axis, by):
    size = lax.axis_size(axis)
    return lax.ppermute(block, axis, [(k, (k + by) % size) for k in range(size)])


def per_device(master_gate, master_up, router_weight, router_gain):
    zs, ys = lax.axis_size("z"), lax.axis_size("y")
    experts, depth, wide = master_gate.shape
    half, own = experts // 2, wide // (zs * ys)
    gate, up = (m.reshape(2, half, depth, wide) for m in (master_gate, master_up))
    gate, up = in_hbm(gate), in_hbm(up)
    weight, gain = in_hbm(router_weight.T), in_hbm(router_gain[None])
    near = pack_ring(gate, weight, gain, zs, ys)
    for dz in RING:
        near[dz] = shifted(near[dz], "z", dz)
    rest = pack_rest(up, zs * ys)
    got_rest = lax.all_to_all(rest, SHARD, 0, 0, tiled=True)
    tiles = [router_tiles(near)] * ys
    for dy in SIDES:
        tiles[dy] = shifted(tiles[dy], "y", dy)
    groups = []
    for batch in BATCHES:
        group = list(regroup([near[dz] for dz in batch], ys))
        for dy in SIDES:
            group[dy] = shifted(group[dy], "y", dy)
        groups += group
    everyone = lax.all_gather(router_rows(tiles), EXPERT, axis=0, tiled=True)
    serve_router = everyone.T
    rows, width = half * own, zs * ys * depth
    ordered = [pltpu.VMEM((ys, zs, rows, LANES), jnp.bfloat16)]
    final_gate = unpack(unpack_ringed_kernel, groups, ordered, rows, width)
    final_up = unpack(unpack_rest_kernel, [got_rest], [], rows, width)
    whole = (experts, own, zs * ys * depth)
    return final_gate.reshape(whole), final_up.reshape(whole), serve_router


def solution(mesh):
    torus = Mesh(mesh.devices.reshape(4, 2, 8, 4), ("x", "core", "z", "y"))
    return jax.shard_map(
        per_device,
        mesh=torus,
        in_specs=(P(EXPERT, SHARD, None), P(EXPERT, SHARD, None), P(SHARD, EXPERT), P(SHARD)),
        out_specs=(P(EXPERT, SHARD, None), P(EXPERT, SHARD, None), P()),
        check_vma=False,
    )
```

time: 134 us -> 121 us (0.903)
  the two profiles are of different devices: /device:TPU:1 before, /device:TPU:8 now
where the time goes in v2:
time: 121 us; the launch traced here: 119 us
  waiting for transfers between devices  46.1 us (38%)
  starting transfers between devices  44.6 us (37%)
  blocking collectives  14.5 us (12%)
  Pallas kernels  10.5 us (9%)
  local copies, waits for them, and re-layouts  2.04 us (2%)
    ppermute x16, waiting for transfers between devices, shifted(): lax.ppermute(block, axis, [(k, (k + by) % size) for k in range(size)])  46.1 us
    ppermute x16, starting transfers between devices, shifted(): lax.ppermute(block, axis, [(k, (k + by) % size) for k in range(size)])  32.9 us
    all_gather x1, blocking collectives, per_device(): everyone = lax.all_gather(router_rows(tiles), EXPERT, axis=0, tiled=True)  14.5 us
    all_to_all x1, starting transfers between devices, per_device(): got_rest = lax.all_to_all(rest, SHARD, 0, 0, tiled=True)  11.7 us
    pallas_call x2, Pallas kernels, pack_for(): pl.pallas_call(functools.partial(kernel, zs, ys, own), in_specs=[HBM] * 3...  3.83 us
    pallas_call x2, Pallas kernels, unpack(): pl.pallas_call(kernel, in_specs=[VMEM] * len(operands), out_specs=HBM, ou...  2.86 us
    pallas_call x1, Pallas kernels, pack_rest(): pl.pallas_call(functools.partial(pack_rest_kernel, shards, own), in_specs...  2.75 us
  transfers between devices with their start and end apart: 17, of which 5 were waited for; matrix products, arithmetic and copies ran while one was open for 2% of the time, Pallas kernels for 5%

profile of v2, /device:TPU:8, one launch (start us, length us, event | category | flops | bytes accessed | tf_op | source)
XLA Modules:
  0.0 118.6 jit_solution(2865399318673807695)
XLA Ops:
  0.6 2.7 %pack_rest.1 = bf16[32,192,128]{2,1,0:T(8,128)(2,1)} custom-call(f32[2,8,64,768]{3,2,1,0:T(8,128)} %bitcast.9), custom_call_target="tpu_custom_call" | custom-call | flops 100000000 | bytes 4718592 | tf_op jit(solution)/shard_map/pack_rest/pallas_call | solution.py:282
  3.4 11.7 %all-to-all-start = ((bf16[32,192,128]{2,1,0:T(8,128)(2,1)}), bf16[32,192,128]{2,1,0:T(8,128)(2,1)S(1)}, u32[]{:S(2)}, u32[]{:S(2)}) async-start(bf16[32,192,128]{2,1,0:T(8,128)(2,1)} %pack_rest.1), calls=%async_computation | async-start | bytes 3145728 | tf_op jit(solution)/shard_map/all_to_all | solution.py:319
  15.1 2.2 %shard_map.67 = (bf16[776,128]{1,0:T(8,128)(2,1)S(1)}, bf16[776,128]{1,0:T(8,128)(2,1)S(1)}, bf16[776,128]{1,0:T(8,128)(2,1)S(1)}, bf16[776,128]{1,0:T(8,128)(2,...) custom-call(f32[2,8,64,768]{3,2,1,0:T(8,128)} %bitcast.7, ...), custom_call_target="tpu_custom_call" | custom-call | flops 100000000 | bytes 3145728 | tf_op jit(solution)/shard_map/pallas_call | solution.py:106
  17.3 3.3 %collective-permute-start.6 = (bf16[776,128]{1,0:T(8,128)(2,1)S(1)}, bf16[776,128]{1,0:T(8,128)(2,1)S(1)}, u32[]{:S(2)}, u32[]{:S(2)}) collective-permute-start(bf16[776,128]{1,0:T(8,128)(2,1)S(1)} %get-tuple-element.25), channel_id=1, source_target_pairs={{0,12},{4,16},{8,20},{12,24},{16,28},{20,0},{24,4},{28,8},{1,13},{... | collective-permute-start | bytes 595976 | tf_op jit(solution)/shard_map/ppermute | solution.py:305
  20.6 1.8 %collective-permute-start.7 = (bf16[776,128]{1,0:T(8,128)(2,1)S(1)}, bf16[776,128]{1,0:T(8,128)(2,1)S(1)}, u32[]{:S(2)}, u32[]{:S(2)}) collective-permute-start(bf16[776,128]{1,0:T(8,128)(2,1)S(1)} %get-tuple-element.26), channel_id=1, source_target_pairs={{0,20},{4,24},{8,28},{12,0},{16,4},{20,8},{24,12},{28,16},{1,21},{... | collective-permute-start | bytes 595976 | tf_op jit(solution)/shard_map/ppermute | solution.py:305
  22.4 2.4 %collective-permute-start.8 = (bf16[776,128]{1,0:T(8,128)(2,1)S(1)}, bf16[776,128]{1,0:T(8,128)(2,1)S(1)}, u32[]{:S(2)}, u32[]{:S(2)}) collective-permute-start(bf16[776,128]{1,0:T(8,128)(2,1)S(1)} %get-tuple-element.27), channel_id=1, source_target_pairs={{0,8},{4,12},{8,16},{12,20},{16,24},{20,28},{24,0},{28,4},{1,9},{5... | collective-permute-start | bytes 595976 | tf_op jit(solution)/shard_map/ppermute | solution.py:305
  24.7 1.8 %collective-permute-start.9 = (bf16[776,128]{1,0:T(8,128)(2,1)S(1)}, bf16[776,128]{1,0:T(8,128)(2,1)S(1)}, u32[]{:S(2)}, u32[]{:S(2)}) collective-permute-start(bf16[776,128]{1,0:T(8,128)(2,1)S(1)} %get-tuple-element.28), channel_id=1, source_target_pairs={{0,24},{4,28},{8,0},{12,4},{16,8},{20,12},{24,16},{28,20},{1,25},{... | collective-permute-start | bytes 595976 | tf_op jit(solution)/shard_map/ppermute | solution.py:305
  26.5 1.7 %shard_map.68 = bf16[776,128]{1,0:T(8,128)(2,1)S(1)} custom-call(f32[2,8,64,768]{3,2,1,0:T(8,128)} %bitcast.8, f32[16,64]{1,0:T(8,128)} %bitcast.14, f32[1,64]{1,0:T(1,128)} %bitcast.16), custom_call_target="tpu_custom_call" | custom-call | flops 100000000 | bytes 3145728 | tf_op jit(solution)/shard_map/pallas_call | solution.py:106
  28.2 5.5 %collective-permute-start = (bf16[776,128]{1,0:T(8,128)(2,1)S(1)}, bf16[776,128]{1,0:T(8,128)(2,1)S(1)}, u32[]{:S(2)}, u32[]{:S(2)}) collective-permute-start(bf16[776,128]{1,0:T(8,128)(2,1)S(1)} %shard_map.68), channel_id=1, source_target_pairs={{0,16},{4,20},{8,24},{12,28},{16,0},{20,4},{24,8},{28,12},{1,17},{... | collective-permute-start | bytes 595976 | tf_op jit(solution)/shard_map/ppermute | solution.py:305
  33.7 32.3 %collective-permute-done.6.refs_0_.refs_3_ = bf16[776,128]{1,0:T(8,128)(2,1)S(1)} collective-permute-done((bf16[776,128]{1,0:T(8,128)(2,1)S(1)}, bf16[776,128]{1,0:T(8,128)(2,1)S(1)}, u32[]{:S(2)}, u32[]{:S(2)}) %collective-permute-start.6) | collective-permute-done | bytes 198688 | tf_op jit(solution)/shard_map/ppermute | solution.py:305
  66.0 2.9 %collective-permute-start.1 = (bf16[776,128]{1,0:T(8,128)(2,1)S(1)}, bf16[776,128]{1,0:T(8,128)(2,1)S(1)}, u32[]{:S(2)}, u32[]{:S(2)}) collective-permute-start(bf16[776,128]{1,0:T(8,128)(2,1)S(1)} %get-tuple-element.19), channel_id=1, source_target_pairs={{0,4},{4,8},{8,12},{12,16},{16,20},{20,24},{24,28},{28,0},{1,5},{5... | collective-permute-start | bytes 595976 | tf_op jit(solution)/shard_map/ppermute | solution.py:305
  68.8 1.6 %collective-permute-start.2 = (bf16[776,128]{1,0:T(8,128)(2,1)S(1)}, bf16[776,128]{1,0:T(8,128)(2,1)S(1)}, u32[]{:S(2)}, u32[]{:S(2)}) collective-permute-start(bf16[776,128]{1,0:T(8,128)(2,1)S(1)} %get-tuple-element.20), channel_id=1, source_target_pairs={{0,28},{4,0},{8,4},{12,8},{16,12},{20,16},{24,20},{28,24},{1,29},{... | collective-permute-start | bytes 595976 | tf_op jit(solution)/shard_map/ppermute | solution.py:305
  70.5 4.8 %collective-permute-done.8.refs_2_ = bf16[776,128]{1,0:T(8,128)(2,1)S(1)} collective-permute-done((bf16[776,128]{1,0:T(8,128)(2,1)S(1)}, bf16[776,128]{1,0:T(8,128)(2,1)S(1)}, u32[]{:S(2)}, u32[]{:S(2)}) %collective-permute-start.8) | collective-permute-done | bytes 198688 | tf_op jit(solution)/shard_map/ppermute | solution.py:305
  75.2 5.9 %collective-permute-done.9.refs_3_.refs_6_ = bf16[776,128]{1,0:T(8,128)(2,1)S(1)} collective-permute-done((bf16[776,128]{1,0:T(8,128)(2,1)S(1)}, bf16[776,128]{1,0:T(8,128)(2,1)S(1)}, u32[]{:S(2)}, u32[]{:S(2)}) %collective-permute-start.9) | collective-permute-done | bytes 198688 | tf_op jit(solution)/shard_map/ppermute | solution.py:305
  81.2 1.5 %collective-permute-start.10 = (bf16[4,192,128]{2,1,0:T(8,128)(2,1)S(1)}, bf16[4,192,128]{2,1,0:T(8,128)(2,1)S(1)}, u32[]{:S(2)}, u32[]{:S(2)}) collective-permute-start(bf16[4,192,128]{2,1,0:T(8,128)(2,1)S(1)} %get-tuple-element.30), channel_id=1, source_target_pairs={{0,1},{1,2},{2,3},{3,0},{4,5},{5,6},{6,7},{7,4},{8,9},{9,10},{10,1... | collective-permute-start | bytes 589832 | tf_op jit(solution)/shard_map/ppermute | solution.py:305
  82.8 2.2 %collective-permute-done.refs_1_.refs_4_ = bf16[776,128]{1,0:T(8,128)(2,1)S(1)} collective-permute-done((bf16[776,128]{1,0:T(8,128)(2,1)S(1)}, bf16[776,128]{1,0:T(8,128)(2,1)S(1)}, u32[]{:S(2)}, u32[]{:S(2)}) %collective-permute-start) | collective-permute-done | bytes 198688 | tf_op jit(solution)/shard_map/ppermute | solution.py:305
  86.5 2.4 %collective-permute-start.14 = (bf16[8,8,128]{2,1,0:T(8,128)(2,1)S(1)}, bf16[8,8,128]{2,1,0:T(8,128)(2,1)S(1)}, u32[]{:S(2)}, u32[]{:S(2)}) collective-permute-start(bf16[8,8,128]{2,1,0:T(8,128)(2,1)S(1)} %router_tiles.1.refs_0_), channel_id=1, source_target_pairs={{0,2},{1,3},{2,0},{3,1},{4,6},{5,7},{6,4},{7,5},{8,10},{9,11},{10,... | collective-permute-start | bytes 49160 | tf_op jit(solution)/shard_map/ppermute | solution.py:305
  88.9 1.8 %collective-permute-start.13 = (bf16[8,8,128]{2,1,0:T(8,128)(2,1)S(1)}, bf16[8,8,128]{2,1,0:T(8,128)(2,1)S(1)}, u32[]{:S(2)}, u32[]{:S(2)}) collective-permute-start(bf16[8,8,128]{2,1,0:T(8,128)(2,1)S(1)} %router_tiles.1.refs_0_), channel_id=1, source_target_pairs={{0,1},{1,2},{2,3},{3,0},{4,5},{5,6},{6,7},{7,4},{8,9},{9,10},{10,1... | collective-permute-start | bytes 49160 | tf_op jit(solution)/shard_map/ppermute | solution.py:305
  90.7 1.4 %collective-permute-start.11 = (bf16[4,192,128]{2,1,0:T(8,128)(2,1)S(1)}, bf16[4,192,128]{2,1,0:T(8,128)(2,1)S(1)}, u32[]{:S(2)}, u32[]{:S(2)}) collective-permute-start(bf16[4,192,128]{2,1,0:T(8,128)(2,1)S(1)} %get-tuple-element.31), channel_id=1, source_target_pairs={{0,2},{1,3},{2,0},{3,1},{4,6},{5,7},{6,4},{7,5},{8,10},{9,11},{10,... | collective-permute-start | bytes 589832 | tf_op jit(solution)/shard_map/ppermute | solution.py:305
  93.6 1.4 %collective-permute-start.3 = (bf16[4,192,128]{2,1,0:T(8,128)(2,1)}, bf16[4,192,128]{2,1,0:T(8,128)(2,1)S(1)}, u32[]{:S(2)}, u32[]{:S(2)}) collective-permute-start(bf16[4,192,128]{2,1,0:T(8,128)(2,1)} %get-tuple-element.22), channel_id=1, source_target_pairs={{0,1},{1,2},{2,3},{3,0},{4,5},{5,6},{6,7},{7,4},{8,9},{9,10},{10,1... | collective-permute-start | bytes 589832 | tf_op jit(solution)/shard_map/ppermute | solution.py:305
  95.0 3.3 %collective-permute-start.4 = (bf16[4,192,128]{2,1,0:T(8,128)(2,1)}, bf16[4,192,128]{2,1,0:T(8,128)(2,1)S(1)}, u32[]{:S(2)}, u32[]{:S(2)}) collective-permute-start(bf16[4,192,128]{2,1,0:T(8,128)(2,1)} %get-tuple-element.23), channel_id=1, source_target_pairs={{0,2},{1,3},{2,0},{3,1},{4,6},{5,7},{6,4},{7,5},{8,10},{9,11},{10,... | collective-permute-start | bytes 589832 | tf_op jit(solution)/shard_map/ppermute | solution.py:305
  99.0 14.5 %all_gather.3 = bf16[128,2048]{1,0:T(8,128)(2,1)} all-gather(bf16[16,2048]{1,0:T(8,128)(2,1)S(1)} %router_rows.1), channel_id=1, replica_groups=mesh['x'=4,'core'=2,'z'=8,'y'=4] {'x','core'}, dimensions={0}, use_global_device_ids=true | all-gather | bytes 589824 | tf_op jit(solution)/shard_map/all_gather | solution.py:329
  113.5 2.0 %copy.7 = bf16[2048,128]{1,0:T(8,128)(2,1)} copy(bf16[2048,128]{0,1:T(8,128)(2,1)} %bitcast.10) | data formatting | bytes 1048576
  115.6 1.5 %shard_map.71 = bf16[2,192,2048]{2,1,0:T(8,128)(2,1)} custom-call(bf16[4,192,128]{2,1,0:T(8,128)(2,1)S(1)} %get-tuple-element.21.refs_0_, bf16[4,192,128]{2,1,0:T(8,128)(2,1)S(1)} %collective-permute-done.3.refs_1_, bf16[4,192,128]{2,1,0:T(8,128)(2,1)S(1)} %collective-permute-done.4.refs_2_, bf16[4,192,128]{2,1,0:T(8,128)(2,1)S(1)} %collective-permute-done.5.refs_3_, ...), custom_call_target="tpu_custom_call" | custom-call | flops 100000000 | bytes 3145728 | tf_op jit(solution)/shard_map/pallas_call | solution.py:222
  (21 shorter events, 5.1 us)
Async XLA Ops:
  3.4 113.7 %all-to-all-start = ((bf16[32,192,128]{2,1,0:T(8,128)(2,1)}), bf16[32,192,128]{2,1,0:T(8,128)(2,1)S(1)}, u32[]{:S(2)}, u32[]{:S(2)}) async-start(bf16[32,192,128]{2,1,0:T(8,128)(2,1)} %pack_rest.1), calls=%async_computation | async-start | bytes 3145728 | tf_op jit(solution)/shard_map/all_to_all | solution.py:319
  17.3 48.7 %collective-permute-start.6 = (bf16[776,128]{1,0:T(8,128)(2,1)S(1)}, bf16[776,128]{1,0:T(8,128)(2,1)S(1)}, u32[]{:S(2)}, u32[]{:S(2)}) collective-permute-start(bf16[776,128]{1,0:T(8,128)(2,1)S(1)} %get-tuple-element.25), channel_id=1, source_target_pairs={{0,12},{4,16},{8,20},{12,24},{16,28},{20,0},{24,4},{28,8},{1,13},{... | collective-permute-start | bytes 595976 | tf_op jit(solution)/shard_map/ppermute | solution.py:305
  20.6 48.2 %collective-permute-start.7 = (bf16[776,128]{1,0:T(8,128)(2,1)S(1)}, bf16[776,128]{1,0:T(8,128)(2,1)S(1)}, u32[]{:S(2)}, u32[]{:S(2)}) collective-permute-start(bf16[776,128]{1,0:T(8,128)(2,1)S(1)} %get-tuple-element.26), channel_id=1, source_target_pairs={{0,20},{4,24},{8,28},{12,0},{16,4},{20,8},{24,12},{28,16},{1,21},{... | collective-permute-start | bytes 595976 | tf_op jit(solution)/shard_map/ppermute | solution.py:305
  22.4 52.9 %collective-permute-start.8 = (bf16[776,128]{1,0:T(8,128)(2,1)S(1)}, bf16[776,128]{1,0:T(8,128)(2,1)S(1)}, u32[]{:S(2)}, u32[]{:S(2)}) collective-permute-start(bf16[776,128]{1,0:T(8,128)(2,1)S(1)} %get-tuple-element.27), channel_id=1, source_target_pairs={{0,8},{4,12},{8,16},{12,20},{16,24},{20,28},{24,0},{28,4},{1,9},{5... | collective-permute-start | bytes 595976 | tf_op jit(solution)/shard_map/ppermute | solution.py:305
  24.7 56.4 %collective-permute-start.9 = (bf16[776,128]{1,0:T(8,128)(2,1)S(1)}, bf16[776,128]{1,0:T(8,128)(2,1)S(1)}, u32[]{:S(2)}, u32[]{:S(2)}) collective-permute-start(bf16[776,128]{1,0:T(8,128)(2,1)S(1)} %get-tuple-element.28), channel_id=1, source_target_pairs={{0,24},{4,28},{8,0},{12,4},{16,8},{20,12},{24,16},{28,20},{1,25},{... | collective-permute-start | bytes 595976 | tf_op jit(solution)/shard_map/ppermute | solution.py:305
  28.2 56.8 %collective-permute-start = (bf16[776,128]{1,0:T(8,128)(2,1)S(1)}, bf16[776,128]{1,0:T(8,128)(2,1)S(1)}, u32[]{:S(2)}, u32[]{:S(2)}) collective-permute-start(bf16[776,128]{1,0:T(8,128)(2,1)S(1)} %shard_map.68), channel_id=1, source_target_pairs={{0,16},{4,20},{8,24},{12,28},{16,0},{20,4},{24,8},{28,12},{1,17},{... | collective-permute-start | bytes 595976 | tf_op jit(solution)/shard_map/ppermute | solution.py:305
  66.0 19.9 %collective-permute-start.1 = (bf16[776,128]{1,0:T(8,128)(2,1)S(1)}, bf16[776,128]{1,0:T(8,128)(2,1)S(1)}, u32[]{:S(2)}, u32[]{:S(2)}) collective-permute-start(bf16[776,128]{1,0:T(8,128)(2,1)S(1)} %get-tuple-element.19), channel_id=1, source_target_pairs={{0,4},{4,8},{8,12},{12,16},{16,20},{20,24},{24,28},{28,0},{1,5},{5... | collective-permute-start | bytes 595976 | tf_op jit(solution)/shard_map/ppermute | solution.py:305
  68.8 17.0 %collective-permute-start.2 = (bf16[776,128]{1,0:T(8,128)(2,1)S(1)}, bf16[776,128]{1,0:T(8,128)(2,1)S(1)}, u32[]{:S(2)}, u32[]{:S(2)}) collective-permute-start(bf16[776,128]{1,0:T(8,128)(2,1)S(1)} %get-tuple-element.20), channel_id=1, source_target_pairs={{0,28},{4,0},{8,4},{12,8},{16,12},{20,16},{24,20},{28,24},{1,29},{... | collective-permute-start | bytes 595976 | tf_op jit(solution)/shard_map/ppermute | solution.py:305
  81.2 17.2 %collective-permute-start.10 = (bf16[4,192,128]{2,1,0:T(8,128)(2,1)S(1)}, bf16[4,192,128]{2,1,0:T(8,128)(2,1)S(1)}, u32[]{:S(2)}, u32[]{:S(2)}) collective-permute-start(bf16[4,192,128]{2,1,0:T(8,128)(2,1)S(1)} %get-tuple-element.30), channel_id=1, source_target_pairs={{0,1},{1,2},{2,3},{3,0},{4,5},{5,6},{6,7},{7,4},{8,9},{9,10},{10,1... | collective-permute-start | bytes 589832 | tf_op jit(solution)/shard_map/ppermute | solution.py:305
  85.9 7.1 %collective-permute-start.15 = (bf16[8,8,128]{2,1,0:T(8,128)(2,1)S(1)}, bf16[8,8,128]{2,1,0:T(8,128)(2,1)S(1)}, u32[]{:S(2)}, u32[]{:S(2)}) collective-permute-start(bf16[8,8,128]{2,1,0:T(8,128)(2,1)S(1)} %router_tiles.1.refs_0_), channel_id=1, source_target_pairs={{0,3},{1,0},{2,1},{3,2},{4,7},{5,4},{6,5},{7,6},{8,11},{9,8},{10,9... | collective-permute-start | bytes 49160 | tf_op jit(solution)/shard_map/ppermute | solution.py:305
  86.5 7.1 %collective-permute-start.14 = (bf16[8,8,128]{2,1,0:T(8,128)(2,1)S(1)}, bf16[8,8,128]{2,1,0:T(8,128)(2,1)S(1)}, u32[]{:S(2)}, u32[]{:S(2)}) collective-permute-start(bf16[8,8,128]{2,1,0:T(8,128)(2,1)S(1)} %router_tiles.1.refs_0_), channel_id=1, source_target_pairs={{0,2},{1,3},{2,0},{3,1},{4,6},{5,7},{6,4},{7,5},{8,10},{9,11},{10,... | collective-permute-start | bytes 49160 | tf_op jit(solution)/shard_map/ppermute | solution.py:305
  88.9 6.1 %collective-permute-start.13 = (bf16[8,8,128]{2,1,0:T(8,128)(2,1)S(1)}, bf16[8,8,128]{2,1,0:T(8,128)(2,1)S(1)}, u32[]{:S(2)}, u32[]{:S(2)}) collective-permute-start(bf16[8,8,128]{2,1,0:T(8,128)(2,1)S(1)} %router_tiles.1.refs_0_), channel_id=1, source_target_pairs={{0,1},{1,2},{2,3},{3,0},{4,5},{5,6},{6,7},{7,4},{8,9},{9,10},{10,1... | collective-permute-start | bytes 49160 | tf_op jit(solution)/shard_map/ppermute | solution.py:305
  90.7 24.9 %collective-permute-start.11 = (bf16[4,192,128]{2,1,0:T(8,128)(2,1)S(1)}, bf16[4,192,128]{2,1,0:T(8,128)(2,1)S(1)}, u32[]{:S(2)}, u32[]{:S(2)}) collective-permute-start(bf16[4,192,128]{2,1,0:T(8,128)(2,1)S(1)} %get-tuple-element.31), channel_id=1, source_target_pairs={{0,2},{1,3},{2,0},{3,1},{4,6},{5,7},{6,4},{7,5},{8,10},{9,11},{10,... | collective-permute-start | bytes 589832 | tf_op jit(solution)/shard_map/ppermute | solution.py:305
  93.0 22.6 %collective-permute-start.12 = (bf16[4,192,128]{2,1,0:T(8,128)(2,1)S(1)}, bf16[4,192,128]{2,1,0:T(8,128)(2,1)S(1)}, u32[]{:S(2)}, u32[]{:S(2)}) collective-permute-start(bf16[4,192,128]{2,1,0:T(8,128)(2,1)S(1)} %get-tuple-element.32), channel_id=1, source_target_pairs={{0,3},{1,0},{2,1},{3,2},{4,7},{5,4},{6,5},{7,6},{8,11},{9,8},{10,9... | collective-permute-start | bytes 589832 | tf_op jit(solution)/shard_map/ppermute | solution.py:305
  93.6 22.0 %collective-permute-start.3 = (bf16[4,192,128]{2,1,0:T(8,128)(2,1)}, bf16[4,192,128]{2,1,0:T(8,128)(2,1)S(1)}, u32[]{:S(2)}, u32[]{:S(2)}) collective-permute-start(bf16[4,192,128]{2,1,0:T(8,128)(2,1)} %get-tuple-element.22), channel_id=1, source_target_pairs={{0,1},{1,2},{2,3},{3,0},{4,5},{5,6},{6,7},{7,4},{8,9},{9,10},{10,1... | collective-permute-start | bytes 589832 | tf_op jit(solution)/shard_map/ppermute | solution.py:305
  95.0 20.6 %collective-permute-start.4 = (bf16[4,192,128]{2,1,0:T(8,128)(2,1)}, bf16[4,192,128]{2,1,0:T(8,128)(2,1)S(1)}, u32[]{:S(2)}, u32[]{:S(2)}) collective-permute-start(bf16[4,192,128]{2,1,0:T(8,128)(2,1)} %get-tuple-element.23), channel_id=1, source_target_pairs={{0,2},{1,3},{2,0},{3,1},{4,6},{5,7},{6,4},{7,5},{8,10},{9,11},{10,... | collective-permute-start | bytes 589832 | tf_op jit(solution)/shard_map/ppermute | solution.py:305
  98.4 17.2 %collective-permute-start.5 = (bf16[4,192,128]{2,1,0:T(8,128)(2,1)}, bf16[4,192,128]{2,1,0:T(8,128)(2,1)S(1)}, u32[]{:S(2)}, u32[]{:S(2)}) collective-permute-start(bf16[4,192,128]{2,1,0:T(8,128)(2,1)} %get-tuple-element.24), channel_id=1, source_target_pairs={{0,3},{1,0},{2,1},{3,2},{4,7},{5,4},{6,5},{7,6},{8,11},{9,8},{10,9... | collective-permute-start | bytes 589832 | tf_op jit(solution)/shard_map/ppermute | solution.py:305

commit v3 on v2

--- a/solution.py
+++ b/solution.py
@@ -20,7 +20,7 @@
 RING = (4, 1, 7, 3, 5, 2, 6)
 BATCHES = ((0, 4, 1, 7), (3, 5, 2, 6))
 LATER = (0,) + RING[1:]
-SIDES = (1, 3, 2)
+SIDES = (2, 1, 3)
 
 
 def cost(size):
@@ -294,6 +294,47 @@
         cost_estimate=cost(6 * up.size),
         name="pack_rest",
     )(up)
+
+
+def router_column_kernel(*refs):
+    xs = len(refs) - 1
+    x = lax.axis_index("x")
+    for k in range(xs):
+        refs[xs][lax.rem(x + xs - k, xs)] = refs[k][...]
+
+
+def router_column(groups):
+    return pl.pallas_call(
+        router_column_kernel,
+        in_specs=[VMEM] * len(groups),
+        out_specs=VMEM,
+        out_shape=packed((len(groups), *groups[0].shape)),
+        compiler_params=GRANT,
+        name="router_column",
+    )(*groups)
+
+
+def whole_router_kernel(mine_ref, other_ref, out_ref, rows_ref):
+    xs, high, _ = mine_ref.shape
+    core = lax.axis_index("core")
+    for x in range(xs):
+        for other, ref in enumerate((mine_ref, other_ref)):
+            group = 2 * x + lax.rem(core + other, 2)
+            rows_ref[pl.ds(pl.multiple_of(group * high, TILE), high), :] = ref[x]
+    out_ref[...] = rows_ref[...].T
+
+
+def whole_router(mine, other):
+    xs, high, depth = mine.shape
+    return pl.pallas_call(
+        whole_router_kernel,
+        in_specs=[VMEM] * 2,
+        out_specs=VMEM,
+        out_shape=packed((depth, 2 * xs * high)),
+        scratch_shapes=[pltpu.VMEM((2 * xs * high, depth), jnp.bfloat16)],
+        compiler_params=GRANT,
+        name="whole_router",
+    )(mine, other)
 
 
 def in_hbm(array):
@@ -326,8 +367,13 @@
         for dy in SIDES:
             group[dy] = shifted(group[dy], "y", dy)
         groups += group
-    everyone = lax.all_gather(router_rows(tiles), EXPERT, axis=0, tiled=True)
-    serve_router = everyone.T
+    rows = router_rows(tiles)
+    columns = [rows] * lax.axis_size("x")
+    for dx in SIDES:
+        columns[dx] = shifted(rows, "x", dx)
+    column = router_column(columns)
+    other = shifted(column, "core", 1)
+    serve_router = whole_router(column, other)
     rows, width = half * own, zs * ys * depth
     ordered = [pltpu.VMEM((ys, zs, rows, LANES), jnp.bfloat16)]
     final_gate = unpack(unpack_ringed_kernel, groups, ordered, rows, width)

time: 121 us -> 125 us (1.033)
  the two profiles are of different devices: /device:TPU:8 before, /device:TPU:1 now
where the time goes in v3:
time: 125 us
  waiting for transfers between devices  62.2 us (50%)
  starting transfers between devices  50.9 us (41%)
  Pallas kernels  10.8 us (9%)
    ppermute x20, waiting for transfers between devices, shifted(): lax.ppermute(block, axis, [(k, (k + by) % size) for k in range(size)])  62.2 us
    ppermute x20, starting transfers between devices, shifted(): lax.ppermute(block, axis, [(k, (k + by) % size) for k in range(size)])  38.8 us
    all_to_all x1, starting transfers between devices, per_device(): got_rest = lax.all_to_all(rest, SHARD, 0, 0, tiled=True)  12 us
    pallas_call x2, Pallas kernels, pack_for(): pl.pallas_call(functools.partial(kernel, zs, ys, own), in_specs=[HBM] * 3...  3.84 us
    pallas_call x2, Pallas kernels, unpack(): pl.pallas_call(kernel, in_specs=[VMEM] * len(operands), out_specs=HBM, ou...  2.86 us
    pallas_call x1, Pallas kernels, pack_rest(): pl.pallas_call(functools.partial(pack_rest_kernel, shards, own), in_specs...  2.75 us
  transfers between devices with their start and end apart: 21, of which 13 were waited for; matrix products, arithmetic and copies ran while one was open for 0% of the time, Pallas kernels for 5%

profile of v3, /device:TPU:1, one launch (start us, length us, event | category | flops | bytes accessed | tf_op | source)
XLA Modules:
  0.0 124.7 jit_solution(16412530697169691237)
XLA Ops:
  0.6 2.7 %pack_rest.1 = bf16[32,192,128]{2,1,0:T(8,128)(2,1)} custom-call(f32[2,8,64,768]{3,2,1,0:T(8,128)} %bitcast.8), custom_call_target="tpu_custom_call" | custom-call | flops 100000000 | bytes 4718592 | tf_op jit(solution)/shard_map/pack_rest/pallas_call | solution.py:282
  3.4 12.0 %all-to-all-start = ((bf16[32,192,128]{2,1,0:T(8,128)(2,1)}), bf16[32,192,128]{2,1,0:T(8,128)(2,1)S(1)}, u32[]{:S(2)}, u32[]{:S(2)}) async-start(bf16[32,192,128]{2,1,0:T(8,128)(2,1)} %pack_rest.1), calls=%async_computation | async-start | bytes 3145728 | tf_op jit(solution)/shard_map/all_to_all | solution.py:360
  15.4 2.2 %shard_map.67 = (bf16[776,128]{1,0:T(8,128)(2,1)S(1)}, bf16[776,128]{1,0:T(8,128)(2,1)S(1)}, bf16[776,128]{1,0:T(8,128)(2,1)S(1)}, bf16[776,128]{1,0:T(8,128)(2,...) custom-call(f32[2,8,64,768]{3,2,1,0:T(8,128)} %bitcast.6, ...), custom_call_target="tpu_custom_call" | custom-call | flops 100000000 | bytes 3145728 | tf_op jit(solution)/shard_map/pallas_call | solution.py:106
  17.6 3.1 %collective-permute-start.6 = (bf16[776,128]{1,0:T(8,128)(2,1)S(1)}, bf16[776,128]{1,0:T(8,128)(2,1)S(1)}, u32[]{:S(2)}, u32[]{:S(2)}) collective-permute-start(bf16[776,128]{1,0:T(8,128)(2,1)S(1)} %get-tuple-element.25), channel_id=1, source_target_pairs={{0,12},{4,16},{8,20},{12,24},{16,28},{20,0},{24,4},{28,8},{1,13},{... | collective-permute-start | bytes 595976 | tf_op jit(solution)/shard_map/ppermute | solution.py:346
  22.1 2.1 %collective-permute-start.8 = (bf16[776,128]{1,0:T(8,128)(2,1)S(1)}, bf16[776,128]{1,0:T(8,128)(2,1)S(1)}, u32[]{:S(2)}, u32[]{:S(2)}) collective-permute-start(bf16[776,128]{1,0:T(8,128)(2,1)S(1)} %get-tuple-element.27), channel_id=1, source_target_pairs={{0,8},{4,12},{8,16},{12,20},{16,24},{20,28},{24,0},{28,4},{1,9},{5... | collective-permute-start | bytes 595976 | tf_op jit(solution)/shard_map/ppermute | solution.py:346
  24.3 1.4 %collective-permute-start.9 = (bf16[776,128]{1,0:T(8,128)(2,1)S(1)}, bf16[776,128]{1,0:T(8,128)(2,1)S(1)}, u32[]{:S(2)}, u32[]{:S(2)}) collective-permute-start(bf16[776,128]{1,0:T(8,128)(2,1)S(1)} %get-tuple-element.28), channel_id=1, source_target_pairs={{0,24},{4,28},{8,0},{12,4},{16,8},{20,12},{24,16},{28,20},{1,25},{... | collective-permute-start | bytes 595976 | tf_op jit(solution)/shard_map/ppermute | solution.py:346
  25.7 1.7 %shard_map.68 = bf16[776,128]{1,0:T(8,128)(2,1)S(1)} custom-call(f32[2,8,64,768]{3,2,1,0:T(8,128)} %bitcast.7, f32[16,64]{1,0:T(8,128)} %bitcast.12, f32[1,64]{1,0:T(1,128)} %bitcast.14), custom_call_target="tpu_custom_call" | custom-call | flops 100000000 | bytes 3145728 | tf_op jit(solution)/shard_map/pallas_call | solution.py:106
  27.4 5.2 %collective-permute-start = (bf16[776,128]{1,0:T(8,128)(2,1)S(1)}, bf16[776,128]{1,0:T(8,128)(2,1)S(1)}, u32[]{:S(2)}, u32[]{:S(2)}) collective-permute-start(bf16[776,128]{1,0:T(8,128)(2,1)S(1)} %shard_map.68), channel_id=1, source_target_pairs={{0,16},{4,20},{8,24},{12,28},{16,0},{20,4},{24,8},{28,12},{1,17},{... | collective-permute-start | bytes 595976 | tf_op jit(solution)/shard_map/ppermute | solution.py:346
  32.6 32.5 %collective-permute-done.6.refs_0_.refs_3_ = bf16[776,128]{1,0:T(8,128)(2,1)S(1)} collective-permute-done((bf16[776,128]{1,0:T(8,128)(2,1)S(1)}, bf16[776,128]{1,0:T(8,128)(2,1)S(1)}, u32[]{:S(2)}, u32[]{:S(2)}) %collective-permute-start.6) | collective-permute-done | bytes 198688 | tf_op jit(solution)/shard_map/ppermute | solution.py:346
  65.2 2.7 %collective-permute-start.2 = (bf16[776,128]{1,0:T(8,128)(2,1)S(1)}, bf16[776,128]{1,0:T(8,128)(2,1)S(1)}, u32[]{:S(2)}, u32[]{:S(2)}) collective-permute-start(bf16[776,128]{1,0:T(8,128)(2,1)S(1)} %get-tuple-element.20), channel_id=1, source_target_pairs={{0,28},{4,0},{8,4},{12,8},{16,12},{20,16},{24,20},{28,24},{1,29},{... | collective-permute-start | bytes 595976 | tf_op jit(solution)/shard_map/ppermute | solution.py:346
  67.9 3.7 %collective-permute-done.8.refs_2_ = bf16[776,128]{1,0:T(8,128)(2,1)S(1)} collective-permute-done((bf16[776,128]{1,0:T(8,128)(2,1)S(1)}, bf16[776,128]{1,0:T(8,128)(2,1)S(1)}, u32[]{:S(2)}, u32[]{:S(2)}) %collective-permute-start.8) | collective-permute-done | bytes 198688 | tf_op jit(solution)/shard_map/ppermute | solution.py:346
  73.0 5.1 %collective-permute-start.11 = (bf16[4,192,128]{2,1,0:T(8,128)(2,1)S(1)}, bf16[4,192,128]{2,1,0:T(8,128)(2,1)S(1)}, u32[]{:S(2)}, u32[]{:S(2)}) collective-permute-start(bf16[4,192,128]{2,1,0:T(8,128)(2,1)S(1)} %get-tuple-element.31), channel_id=1, source_target_pairs={{0,2},{1,3},{2,0},{3,1},{4,6},{5,7},{6,4},{7,5},{8,10},{9,11},{10,... | collective-permute-start | bytes 589832 | tf_op jit(solution)/shard_map/ppermute | solution.py:346
  78.0 2.6 %collective-permute-done.refs_1_.refs_4_ = bf16[776,128]{1,0:T(8,128)(2,1)S(1)} collective-permute-done((bf16[776,128]{1,0:T(8,128)(2,1)S(1)}, bf16[776,128]{1,0:T(8,128)(2,1)S(1)}, u32[]{:S(2)}, u32[]{:S(2)}) %collective-permute-start) | collective-permute-done | bytes 198688 | tf_op jit(solution)/shard_map/ppermute | solution.py:346
  80.6 5.3 %collective-permute-done.1.refs_2_.refs_1_ = bf16[776,128]{1,0:T(8,128)(2,1)S(1)} collective-permute-done((bf16[776,128]{1,0:T(8,128)(2,1)S(1)}, bf16[776,128]{1,0:T(8,128)(2,1)S(1)}, u32[]{:S(2)}, u32[]{:S(2)}) %collective-permute-start.1) | collective-permute-done | bytes 198688 | tf_op jit(solution)/shard_map/ppermute | solution.py:346
  86.0 2.6 %collective-permute-start.15 = (bf16[8,8,128]{2,1,0:T(8,128)(2,1)S(1)}, bf16[8,8,128]{2,1,0:T(8,128)(2,1)S(1)}, u32[]{:S(2)}, u32[]{:S(2)}) collective-permute-start(bf16[8,8,128]{2,1,0:T(8,128)(2,1)S(1)} %router_tiles.1.refs_0_), channel_id=1, source_target_pairs={{0,3},{1,0},{2,1},{3,2},{4,7},{5,4},{6,5},{7,6},{8,11},{9,8},{10,9... | collective-permute-start | bytes 49160 | tf_op jit(solution)/shard_map/ppermute | solution.py:346
  89.8 2.9 %collective-permute-done.14.refs_2_ = bf16[8,8,128]{2,1,0:T(8,128)(2,1)S(1)} collective-permute-done((bf16[8,8,128]{2,1,0:T(8,128)(2,1)S(1)}, bf16[8,8,128]{2,1,0:T(8,128)(2,1)S(1)}, u32[]{:S(2)}, u32[]{:S(2)}) %collective-permute-start.14) | collective-permute-done | bytes 16416 | tf_op jit(solution)/shard_map/ppermute | solution.py:346
  93.0 2.7 %collective-permute-start.18 = (bf16[16,2048]{1,0:T(8,128)(2,1)S(1)}, bf16[16,2048]{1,0:T(8,128)(2,1)S(1)}, u32[]{:S(2)}, u32[]{:S(2)}) collective-permute-start(bf16[16,2048]{1,0:T(8,128)(2,1)S(1)} %router_rows.1.refs_0_), channel_id=1, source_target_pairs={{0,192},{64,0},{128,64},{192,128},{1,193},{65,1},{129,65},{193,129... | collective-permute-start | bytes 196616 | tf_op jit(solution)/shard_map/ppermute | solution.py:346
  97.1 3.3 %collective-permute-done.17.refs_2_ = bf16[16,2048]{1,0:T(8,128)(2,1)S(1)} collective-permute-done((bf16[16,2048]{1,0:T(8,128)(2,1)S(1)}, bf16[16,2048]{1,0:T(8,128)(2,1)S(1)}, u32[]{:S(2)}, u32[]{:S(2)}) %collective-permute-start.17) | collective-permute-done | bytes 65568 | tf_op jit(solution)/shard_map/ppermute | solution.py:346
  101.1 4.6 %collective-permute-start.19 = (bf16[4,16,2048]{2,1,0:T(8,128)(2,1)S(1)}, bf16[4,16,2048]{2,1,0:T(8,128)(2,1)S(1)}, u32[]{:S(2)}, u32[]{:S(2)}) collective-permute-start(bf16[4,16,2048]{2,1,0:T(8,128)(2,1)S(1)} %router_column.1.mine_ref), channel_id=1, source_target_pairs={{0,32},{32,0},{1,33},{33,1},{2,34},{34,2},{3,35},{35,3},{4,36},{36... | collective-permute-start | bytes 786440 | tf_op jit(solution)/shard_map/ppermute | solution.py:346
  105.8 1.5 %collective-permute-start.3 = (bf16[4,192,128]{2,1,0:T(8,128)(2,1)S(1)}, bf16[4,192,128]{2,1,0:T(8,128)(2,1)S(1)}, u32[]{:S(2)}, u32[]{:S(2)}) collective-permute-start(bf16[4,192,128]{2,1,0:T(8,128)(2,1)S(1)} %get-tuple-element.22), channel_id=1, source_target_pairs={{0,1},{1,2},{2,3},{3,0},{4,5},{5,6},{6,7},{7,4},{8,9},{9,10},{10,1... | collective-permute-start | bytes 589832 | tf_op jit(solution)/shard_map/ppermute | solution.py:346
  109.9 2.3 %collective-permute-done.12.refs_7_ = bf16[4,192,128]{2,1,0:T(8,128)(2,1)S(1)} collective-permute-done((bf16[4,192,128]{2,1,0:T(8,128)(2,1)S(1)}, bf16[4,192,128]{2,1,0:T(8,128)(2,1)S(1)}, u32[]{:S(2)}, u32[]{:S(2)}) %collective-permute-start.12) | collective-permute-done | bytes 196640 | tf_op jit(solution)/shard_map/ppermute | solution.py:346
  113.2 4.2 %collective-permute-done.4.refs_2_ = bf16[4,192,128]{2,1,0:T(8,128)(2,1)S(1)} collective-permute-done((bf16[4,192,128]{2,1,0:T(8,128)(2,1)S(1)}, bf16[4,192,128]{2,1,0:T(8,128)(2,1)S(1)}, u32[]{:S(2)}, u32[]{:S(2)}) %collective-permute-start.4) | collective-permute-done | bytes 196640 | tf_op jit(solution)/shard_map/ppermute | solution.py:346
  117.4 3.2 %collective-permute-done.5.refs_3_ = bf16[4,192,128]{2,1,0:T(8,128)(2,1)S(1)} collective-permute-done((bf16[4,192,128]{2,1,0:T(8,128)(2,1)S(1)}, bf16[4,192,128]{2,1,0:T(8,128)(2,1)S(1)}, u32[]{:S(2)}, u32[]{:S(2)}) %collective-permute-start.5) | collective-permute-done | bytes 196640 | tf_op jit(solution)/shard_map/ppermute | solution.py:346
  120.6 1.5 %shard_map.71 = bf16[2,192,2048]{2,1,0:T(8,128)(2,1)} custom-call(bf16[4,192,128]{2,1,0:T(8,128)(2,1)S(1)} %get-tuple-element.21.refs_0_, bf16[4,192,128]{2,1,0:T(8,128)(2,1)S(1)} %collective-permute-done.3.refs_1_, bf16[4,192,128]{2,1,0:T(8,128)(2,1)S(1)} %collective-permute-done.4.refs_2_, bf16[4,192,128]{2,1,0:T(8,128)(2,1)S(1)} %collective-permute-done.5.refs_3_, ...), custom_call_target="tpu_custom_call" | custom-call | flops 100000000 | bytes 3145728 | tf_op jit(solution)/shard_map/pallas_call | solution.py:222
  (29 shorter events, 12.5 us)
Async XLA Ops:
  3.4 119.8 %all-to-all-start = ((bf16[32,192,128]{2,1,0:T(8,128)(2,1)}), bf16[32,192,128]{2,1,0:T(8,128)(2,1)S(1)}, u32[]{:S(2)}, u32[]{:S(2)}) async-start(bf16[32,192,128]{2,1,0:T(8,128)(2,1)} %pack_rest.1), calls=%async_computation | async-start | bytes 3145728 | tf_op jit(solution)/shard_map/all_to_all | solution.py:360
  17.6 47.6 %collective-permute-start.6 = (bf16[776,128]{1,0:T(8,128)(2,1)S(1)}, bf16[776,128]{1,0:T(8,128)(2,1)S(1)}, u32[]{:S(2)}, u32[]{:S(2)}) collective-permute-start(bf16[776,128]{1,0:T(8,128)(2,1)S(1)} %get-tuple-element.25), channel_id=1, source_target_pairs={{0,12},{4,16},{8,20},{12,24},{16,28},{20,0},{24,4},{28,8},{1,13},{... | collective-permute-start | bytes 595976 | tf_op jit(solution)/shard_map/ppermute | solution.py:346
  20.7 44.5 %collective-permute-start.7 = (bf16[776,128]{1,0:T(8,128)(2,1)S(1)}, bf16[776,128]{1,0:T(8,128)(2,1)S(1)}, u32[]{:S(2)}, u32[]{:S(2)}) collective-permute-start(bf16[776,128]{1,0:T(8,128)(2,1)S(1)} %get-tuple-element.26), channel_id=1, source_target_pairs={{0,20},{4,24},{8,28},{12,0},{16,4},{20,8},{24,12},{28,16},{1,21},{... | collective-permute-start | bytes 595976 | tf_op jit(solution)/shard_map/ppermute | solution.py:346
  22.1 49.4 %collective-permute-start.8 = (bf16[776,128]{1,0:T(8,128)(2,1)S(1)}, bf16[776,128]{1,0:T(8,128)(2,1)S(1)}, u32[]{:S(2)}, u32[]{:S(2)}) collective-permute-start(bf16[776,128]{1,0:T(8,128)(2,1)S(1)} %get-tuple-element.27), channel_id=1, source_target_pairs={{0,8},{4,12},{8,16},{12,20},{16,24},{20,28},{24,0},{28,4},{1,9},{5... | collective-permute-start | bytes 595976 | tf_op jit(solution)/shard_map/ppermute | solution.py:346
  24.3 47.2 %collective-permute-start.9 = (bf16[776,128]{1,0:T(8,128)(2,1)S(1)}, bf16[776,128]{1,0:T(8,128)(2,1)S(1)}, u32[]{:S(2)}, u32[]{:S(2)}) collective-permute-start(bf16[776,128]{1,0:T(8,128)(2,1)S(1)} %get-tuple-element.28), channel_id=1, source_target_pairs={{0,24},{4,28},{8,0},{12,4},{16,8},{20,12},{24,16},{28,20},{1,25},{... | collective-permute-start | bytes 595976 | tf_op jit(solution)/shard_map/ppermute | solution.py:346
  27.4 53.2 %collective-permute-start = (bf16[776,128]{1,0:T(8,128)(2,1)S(1)}, bf16[776,128]{1,0:T(8,128)(2,1)S(1)}, u32[]{:S(2)}, u32[]{:S(2)}) collective-permute-start(bf16[776,128]{1,0:T(8,128)(2,1)S(1)} %shard_map.68), channel_id=1, source_target_pairs={{0,16},{4,20},{8,24},{12,28},{16,0},{20,4},{24,8},{28,12},{1,17},{... | collective-permute-start | bytes 595976 | tf_op jit(solution)/shard_map/ppermute | solution.py:346
  65.2 20.8 %collective-permute-start.1 = (bf16[776,128]{1,0:T(8,128)(2,1)S(1)}, bf16[776,128]{1,0:T(8,128)(2,1)S(1)}, u32[]{:S(2)}, u32[]{:S(2)}) collective-permute-start(bf16[776,128]{1,0:T(8,128)(2,1)S(1)} %get-tuple-element.19), channel_id=1, source_target_pairs={{0,4},{4,8},{8,12},{12,16},{16,20},{20,24},{24,28},{28,0},{1,5},{5... | collective-permute-start | bytes 595976 | tf_op jit(solution)/shard_map/ppermute | solution.py:346
  65.2 20.8 %collective-permute-start.2 = (bf16[776,128]{1,0:T(8,128)(2,1)S(1)}, bf16[776,128]{1,0:T(8,128)(2,1)S(1)}, u32[]{:S(2)}, u32[]{:S(2)}) collective-permute-start(bf16[776,128]{1,0:T(8,128)(2,1)S(1)} %get-tuple-element.20), channel_id=1, source_target_pairs={{0,28},{4,0},{8,4},{12,8},{16,12},{20,16},{24,20},{28,24},{1,29},{... | collective-permute-start | bytes 595976 | tf_op jit(solution)/shard_map/ppermute | solution.py:346
  71.6 35.8 %collective-permute-start.10 = (bf16[4,192,128]{2,1,0:T(8,128)(2,1)S(1)}, bf16[4,192,128]{2,1,0:T(8,128)(2,1)S(1)}, u32[]{:S(2)}, u32[]{:S(2)}) collective-permute-start(bf16[4,192,128]{2,1,0:T(8,128)(2,1)S(1)} %get-tuple-element.30), channel_id=1, source_target_pairs={{0,1},{1,2},{2,3},{3,0},{4,5},{5,6},{6,7},{7,4},{8,9},{9,10},{10,1... | collective-permute-start | bytes 589832 | tf_op jit(solution)/shard_map/ppermute | solution.py:346
  73.0 35.6 %collective-permute-start.11 = (bf16[4,192,128]{2,1,0:T(8,128)(2,1)S(1)}, bf16[4,192,128]{2,1,0:T(8,128)(2,1)S(1)}, u32[]{:S(2)}, u32[]{:S(2)}) collective-permute-start(bf16[4,192,128]{2,1,0:T(8,128)(2,1)S(1)} %get-tuple-element.31), channel_id=1, source_target_pairs={{0,2},{1,3},{2,0},{3,1},{4,6},{5,7},{6,4},{7,5},{8,10},{9,11},{10,... | collective-permute-start | bytes 589832 | tf_op jit(solution)/shard_map/ppermute | solution.py:346
  86.0 3.8 %collective-permute-start.15 = (bf16[8,8,128]{2,1,0:T(8,128)(2,1)S(1)}, bf16[8,8,128]{2,1,0:T(8,128)(2,1)S(1)}, u32[]{:S(2)}, u32[]{:S(2)}) collective-permute-start(bf16[8,8,128]{2,1,0:T(8,128)(2,1)S(1)} %router_tiles.1.refs_0_), channel_id=1, source_target_pairs={{0,3},{1,0},{2,1},{3,2},{4,7},{5,4},{6,5},{7,6},{8,11},{9,8},{10,9... | collective-permute-start | bytes 49160 | tf_op jit(solution)/shard_map/ppermute | solution.py:346
  88.6 4.1 %collective-permute-start.14 = (bf16[8,8,128]{2,1,0:T(8,128)(2,1)S(1)}, bf16[8,8,128]{2,1,0:T(8,128)(2,1)S(1)}, u32[]{:S(2)}, u32[]{:S(2)}) collective-permute-start(bf16[8,8,128]{2,1,0:T(8,128)(2,1)S(1)} %router_tiles.1.refs_0_), channel_id=1, source_target_pairs={{0,2},{1,3},{2,0},{3,1},{4,6},{5,7},{6,4},{7,5},{8,10},{9,11},{10,... | collective-permute-start | bytes 49160 | tf_op jit(solution)/shard_map/ppermute | solution.py:346
  89.1 3.8 %collective-permute-start.13 = (bf16[8,8,128]{2,1,0:T(8,128)(2,1)S(1)}, bf16[8,8,128]{2,1,0:T(8,128)(2,1)S(1)}, u32[]{:S(2)}, u32[]{:S(2)}) collective-permute-start(bf16[8,8,128]{2,1,0:T(8,128)(2,1)S(1)} %router_tiles.1.refs_0_), channel_id=1, source_target_pairs={{0,1},{1,2},{2,3},{3,0},{4,5},{5,6},{6,7},{7,4},{8,9},{9,10},{10,1... | collective-permute-start | bytes 49160 | tf_op jit(solution)/shard_map/ppermute | solution.py:346
  93.0 4.1 %collective-permute-start.18 = (bf16[16,2048]{1,0:T(8,128)(2,1)S(1)}, bf16[16,2048]{1,0:T(8,128)(2,1)S(1)}, u32[]{:S(2)}, u32[]{:S(2)}) collective-permute-start(bf16[16,2048]{1,0:T(8,128)(2,1)S(1)} %router_rows.1.refs_0_), channel_id=1, source_target_pairs={{0,192},{64,0},{128,64},{192,128},{1,193},{65,1},{129,65},{193,129... | collective-permute-start | bytes 196616 | tf_op jit(solution)/shard_map/ppermute | solution.py:346
  95.8 4.7 %collective-permute-start.17 = (bf16[16,2048]{1,0:T(8,128)(2,1)S(1)}, bf16[16,2048]{1,0:T(8,128)(2,1)S(1)}, u32[]{:S(2)}, u32[]{:S(2)}) collective-permute-start(bf16[16,2048]{1,0:T(8,128)(2,1)S(1)} %router_rows.1.refs_0_), channel_id=1, source_target_pairs={{0,128},{64,192},{128,0},{192,64},{1,129},{65,193},{129,1},{193,65... | collective-permute-start | bytes 196616 | tf_op jit(solution)/shard_map/ppermute | solution.py:346
  96.3 4.8 %collective-permute-start.16 = (bf16[16,2048]{1,0:T(8,128)(2,1)S(1)}, bf16[16,2048]{1,0:T(8,128)(2,1)S(1)}, u32[]{:S(2)}, u32[]{:S(2)}) collective-permute-start(bf16[16,2048]{1,0:T(8,128)(2,1)S(1)} %router_rows.1.refs_0_), channel_id=1, source_target_pairs={{0,64},{64,128},{128,192},{192,0},{1,65},{65,129},{129,193},{193,1... | collective-permute-start | bytes 196616 | tf_op jit(solution)/shard_map/ppermute | solution.py:346
  101.1 21.0 %collective-permute-start.19 = (bf16[4,16,2048]{2,1,0:T(8,128)(2,1)S(1)}, bf16[4,16,2048]{2,1,0:T(8,128)(2,1)S(1)}, u32[]{:S(2)}, u32[]{:S(2)}) collective-permute-start(bf16[4,16,2048]{2,1,0:T(8,128)(2,1)S(1)} %router_column.1.mine_ref), channel_id=1, source_target_pairs={{0,32},{32,0},{1,33},{33,1},{2,34},{34,2},{3,35},{35,3},{4,36},{36... | collective-permute-start | bytes 786440 | tf_op jit(solution)/shard_map/ppermute | solution.py:346
  105.8 6.4 %collective-permute-start.12 = (bf16[4,192,128]{2,1,0:T(8,128)(2,1)S(1)}, bf16[4,192,128]{2,1,0:T(8,128)(2,1)S(1)}, u32[]{:S(2)}, u32[]{:S(2)}) collective-permute-start(bf16[4,192,128]{2,1,0:T(8,128)(2,1)S(1)} %get-tuple-element.32), channel_id=1, source_target_pairs={{0,3},{1,0},{2,1},{3,2},{4,7},{5,4},{6,5},{7,6},{8,11},{9,8},{10,9... | collective-permute-start | bytes 589832 | tf_op jit(solution)/shard_map/ppermute | solution.py:346
  105.8 7.4 %collective-permute-start.3 = (bf16[4,192,128]{2,1,0:T(8,128)(2,1)S(1)}, bf16[4,192,128]{2,1,0:T(8,128)(2,1)S(1)}, u32[]{:S(2)}, u32[]{:S(2)}) collective-permute-start(bf16[4,192,128]{2,1,0:T(8,128)(2,1)S(1)} %get-tuple-element.22), channel_id=1, source_target_pairs={{0,1},{1,2},{2,3},{3,0},{4,5},{5,6},{6,7},{7,4},{8,9},{9,10},{10,1... | collective-permute-start | bytes 589832 | tf_op jit(solution)/shard_map/ppermute | solution.py:346
  107.4 10.0 %collective-permute-start.4 = (bf16[4,192,128]{2,1,0:T(8,128)(2,1)S(1)}, bf16[4,192,128]{2,1,0:T(8,128)(2,1)S(1)}, u32[]{:S(2)}, u32[]{:S(2)}) collective-permute-start(bf16[4,192,128]{2,1,0:T(8,128)(2,1)S(1)} %get-tuple-element.23), channel_id=1, source_target_pairs={{0,2},{1,3},{2,0},{3,1},{4,6},{5,7},{6,4},{7,5},{8,10},{9,11},{10,... | collective-permute-start | bytes 589832 | tf_op jit(solution)/shard_map/ppermute | solution.py:346
  108.6 12.0 %collective-permute-start.5 = (bf16[4,192,128]{2,1,0:T(8,128)(2,1)S(1)}, bf16[4,192,128]{2,1,0:T(8,128)(2,1)S(1)}, u32[]{:S(2)}, u32[]{:S(2)}) collective-permute-start(bf16[4,192,128]{2,1,0:T(8,128)(2,1)S(1)} %get-tuple-element.24), channel_id=1, source_target_pairs={{0,3},{1,0},{2,1},{3,2},{4,7},{5,4},{6,5},{7,6},{8,11},{9,8},{10,9... | collective-permute-start | bytes 589832 | tf_op jit(solution)/shard_map/ppermute | solution.py:346
